TPU v7x, 8 devices: a whole 2x2x1 slice. The times are simulated.
8 devices in a mesh: dp: 1 (over z), sx: 2 (over y), sy: 4 (over x, core).
Axes of the slice: x: 2, y: 2, z: 1, core: 2. Of those that a mesh axis runs over, the one named last changes fastest.
Arguments:
- act_in: bfloat16 [16, 1024, 16, 256], P('dp', 'sy', 'sx')
- norm_first: bfloat16 [2, 256], replicated
- w_first: bfloat16 [3, 3, 256, 128], replicated
- w_short: bfloat16 [256, 128], replicated
- norm_rest: bfloat16 [6, 2, 128], replicated
- w_rest: bfloat16 [5, 3, 3, 128, 128], replicated
- bias_rest: bfloat16 [7, 128], replicated
- w_out: bfloat16 [3, 3, 128, 3], replicated
- bias_out: bfloat16 [3], replicated
Outputs:
- output: float32 [16, 1024, 16, 3], P('dp', 'sy', 'sx')
All inputs are finite; a program needn't handle non-finite values.
Results may differ from a plain program's by a relative error of at most 0.00879114.
Values are sent between devices in bfloat16 or wider.
A program may use at most 1 GiB of HBM per device.

v0:
```python
import jax
import jax.numpy as jnp
from jax import lax
from jax.sharding import PartitionSpec as P

GROUPS = 32
GN_EPS = 1e-6


def solution(mesh):
    rows_n = mesh.shape["sy"]
    cols_n = mesh.shape["sx"]
    to_below = [(position, position + 1) for position in range(rows_n - 1)]
    to_above = [(position + 1, position) for position in range(rows_n - 1)]
    to_right = [(position, position + 1) for position in range(cols_n - 1)]
    to_left = [(position + 1, position) for position in range(cols_n - 1)]
    tile_spec = P("dp", "sy", "sx", None)
    replicated = P()

    def add_border(act_map):
        top_row = lax.ppermute(act_map[:, -1:], "sy", to_below)
        bottom_row = lax.ppermute(act_map[:, :1], "sy", to_above)
        tall = jnp.concatenate([top_row, act_map, bottom_row], axis=1)
        left_col = lax.ppermute(tall[:, :, -1:], "sx", to_right)
        right_col = lax.ppermute(tall[:, :, :1], "sx", to_left)
        return jnp.concatenate([left_col, tall, right_col], axis=2)

    def conv_tile(act_map, kernel):
        return lax.conv_general_dilated(add_border(act_map), kernel, (1, 1), ((0, 0), (0, 0)), dimension_numbers=("NHWC", "HWIO", "NHWC"), preferred_element_type=jnp.float32)

    def group_norm_act(act_map, norm_pair):
        samples = act_map.shape[0]
        per_group = act_map.shape[3] // GROUPS
        group_count = act_map.shape[1] * rows_n * act_map.shape[2] * cols_n * per_group
        sum_one = jnp.sum(act_map, axis=(1, 2), dtype=jnp.float32).reshape(samples, GROUPS, per_group).sum(axis=2)
        sum_two = jnp.sum(jnp.square(act_map.astype(jnp.float32)), axis=(1, 2)).reshape(samples, GROUPS, per_group).sum(axis=2)
        totals = lax.psum(jnp.stack([sum_one, sum_two], axis=-1), ("sy", "sx"))
        group_mean = totals[:, :, 0] / group_count
        inv_std = lax.rsqrt(totals[:, :, 1] / group_count - group_mean * group_mean + GN_EPS)
        chan_scale = jnp.repeat(inv_std, per_group, axis=1) * norm_pair[0].astype(jnp.float32)
        chan_shift = norm_pair[1].astype(jnp.float32) - jnp.repeat(group_mean, per_group, axis=1) * chan_scale
        return jax.nn.silu(act_map.astype(jnp.float32) * chan_scale[:, None, None, :] + chan_shift[:, None, None, :]).astype(jnp.bfloat16)

    def local_decode(act_in, norm_first, w_first, w_short, norm_rest, w_rest, bias_rest, w_out, bias_out):
        bias_rows = bias_rest.astype(jnp.float32)
        mid_act = (conv_tile(group_norm_act(act_in, norm_first), w_first) + bias_rows[0]).astype(jnp.bfloat16)
        skip_path = jnp.einsum("nhwc,cd->nhwd", act_in, w_short, preferred_element_type=jnp.float32) + bias_rows[6]
        hidden = (conv_tile(group_norm_act(mid_act, norm_rest[0]), w_rest[0]) + bias_rows[1] + skip_path).astype(jnp.bfloat16)
        for res_index in range(1, 3):
            first_at = 2 * res_index - 1
            mid_act = (conv_tile(group_norm_act(hidden, norm_rest[first_at]), w_rest[first_at]) + bias_rows[first_at + 1]).astype(jnp.bfloat16)
            hidden = (conv_tile(group_norm_act(mid_act, norm_rest[first_at + 1]), w_rest[first_at + 1]) + bias_rows[first_at + 2] + hidden.astype(jnp.float32)).astype(jnp.bfloat16)
        return conv_tile(group_norm_act(hidden, norm_rest[5]), w_out) + bias_out.astype(jnp.float32)

    return jax.shard_map(local_decode, mesh=mesh, in_specs=(tile_spec, replicated, replicated, replicated, replicated, replicated, replicated, replicated, replicated), out_specs=tile_spec, check_vma=False)
```

profile of v0, /device:TPU:0, one launch (start us, length us, event | category | flops | bytes accessed | tf_op | source)
XLA Modules:
  0.0 811.5 jit_solution(9115829805051289771)
XLA Ops:
  0.0 29.6 %convert_reduce_fusion = (f32[16,256]{1,0:T(8,128)S(1)}, f32[16,256]{1,0:T(8,128)S(1)}) fusion(bf16[16,256,8,256]{3,2,1,0:T(8,128)(2,1)} %param.9), kind=kLoop, calls=%fused_computation.2 | loop fusion | flops 33546240 | bytes 16809984 | tf_op jit(solution)/shard_map/reduce_sum | solution.py:35
  29.9 25.2 %psum.49 = f32[16,32,2]{0,1,2:T(8,128)S(1)} all-reduce(f32[16,32,2]{0,1,2:T(8,128)S(1)} %pad_maximum_fusion.21), channel_id=1, replica_groups=mesh['dp'=1,'sx'=2,'sy'=4] {'sy','sx'}, use_global_device_ids=true, to_apply=%region_4.0 | all-reduce | flops 1024 | bytes 8192 | tf_op jit(solution)/shard_map/psum | solution.py:37
  55.4 30.9 %fusion.7 = bf16[16,256,8,256]{3,0,2,1:T(8,128)(2,1)S(1)} fusion(f32[16,256]{1,0:T(8,128)S(1)} %get-tuple-element.31, f32[16,256]{1,0:T(8,128)S(1)} %get-tuple-element.32, bf16[16,256,8,256]{3,2,1,0:T(8,128)(2,1)} %param.9), kind=kLoop, calls=%fused_computation.10 | loop fusion | flops 67108864 | bytes 33587200 | tf_op jit(solution)/shard_map/convert_element_type | solution.py:42
  88.9 4.3 collective-permute-done.1
  99.1 41.6 %collective-permute-done.2 = bf16[16,258,1,256]{3,0,2,1:T(8,128)(2,1)S(1)} collective-permute-done((bf16[16,258,1,256]{3,0,2,1:T(8,128)(2,1)S(1)}, bf16[16,258,1,256]{3,0,2,1:T(8,128)(2,1)S(1)}, u32[]{:S(2)}, u32[]{:S(2)}) %collective-permute-start.2) | collective-permute-done | bytes 2113568 | tf_op jit(solution)/shard_map/ppermute | solution.py:24
  140.7 4.8 collective-permute-done.3
  145.5 42.3 %convert_reduce_fusion.6 = (f32[16,128]{1,0:T(8,128)S(1)}, f32[16,128]{1,0:T(8,128)S(1)}, bf16[16,256,8,128]{3,0,2,1:T(8,128)(2,1)}) fusion(f32[128]{0:T(128)S(1)} %get-tuple-element.67, bf16[3,3,256,128]{3,2,1,0:T(8,128)(2,1)S(1)} %copy-done, bf16[16,258,1,256]{3,0,2,1:T(8,128)(2,1)S(1)} %collective-permute-done.3, ...), kind=kOutput, calls=%fused_computation.30 | convolution fusion | flops 19394785280 | bytes 30130688 | tf_op jit(solution)/shard_map/conv_general_dilated | solution.py:29
  188.1 22.4 %psum.50 = f32[16,32,2]{0,1,2:T(8,128)S(1)} all-reduce(f32[16,32,2]{0,1,2:T(8,128)S(1)} %pad_maximum_fusion.22), channel_id=1, replica_groups=mesh['dp'=1,'sx'=2,'sy'=4] {'sy','sx'}, use_global_device_ids=true, to_apply=%region_9.10 | all-reduce | flops 1024 | bytes 8192 | tf_op jit(solution)/shard_map/psum | solution.py:37
  210.7 7.0 fusion.25
  220.4 4.3 collective-permute-done.5
  224.9 3.5 collective-permute-start.6
  230.3 21.3 %fusion.68 = f32[16,256,8,128]{3,0,2,1:T(8,128)} fusion(bf16[16,256,8,256]{3,2,1,0:T(8,128)(2,1)} %param.9, bf16[256,128]{1,0:T(8,128)(2,1)S(1)} %copy-done.3), kind=kOutput, calls=%fused_computation.95 | convolution fusion | flops 2147483648 | bytes 33619968 | tf_op jit(solution)/shard_map/nhwc,cd->nhwd/dot_general | solution.py:47
  251.6 3.7 collective-permute-done.7
  255.3 25.7 %convert_reduce_fusion.2 = (f32[16,128]{1,0:T(8,128)S(1)}, f32[16,128]{1,0:T(8,128)S(1)}, bf16[16,256,8,128]{3,0,2,1:T(8,128)(2,1)}) fusion(f32[16,256,8,128]{3,0,2,1:T(8,128)} %fusion.68, f32[128]{0:T(128)S(1)} %get-tuple-element.65, f32[128]{0:T(128)S(1)} %get-tuple-element.66, bf16[5,3,3,128,128]{4,3,2,1,0:T(8,128)(2,1)S(1)} %copy-done.18, ...), kind=kOutput, calls=%fused_computation.18 | convolution fusion | flops 9718362112 | bytes 36045824 | tf_op jit(solution)/shard_map/conv_general_dilated | solution.py:29
  281.4 22.4 %psum.51 = f32[16,32,2]{0,1,2:T(8,128)S(1)} all-reduce(f32[16,32,2]{0,1,2:T(8,128)S(1)} %pad_maximum_fusion.23), channel_id=1, replica_groups=mesh['dp'=1,'sx'=2,'sy'=4] {'sy','sx'}, use_global_device_ids=true, to_apply=%region_14.15 | all-reduce | flops 1024 | bytes 8192 | tf_op jit(solution)/shard_map/psum | solution.py:37
  304.0 7.0 fusion.57
  313.6 4.3 collective-permute-done.9
  318.2 3.2 collective-permute-start.10
  322.7 20.7 %collective-permute-done.10 = bf16[16,258,1,128]{3,0,2,1:T(8,128)(2,1)S(1)} collective-permute-done((bf16[16,258,1,128]{3,0,2,1:T(8,128)(2,1)S(1)}, bf16[16,258,1,128]{3,0,2,1:T(8,128)(2,1)S(1)}, u32[]{:S(2)}, u32[]{:S(2)}) %collective-permute-start.10) | collective-permute-done | bytes 1056800 | tf_op jit(solution)/shard_map/ppermute | solution.py:24
  343.4 4.8 collective-permute-done.11
  348.2 22.0 %convert_reduce_fusion.5 = (f32[16,128]{1,0:T(8,128)S(1)}, f32[16,128]{1,0:T(8,128)S(1)}, bf16[16,256,8,128]{3,0,2,1:T(8,128)(2,1)}) fusion(f32[128]{0:T(128)S(1)} %get-tuple-element.64, bf16[5,3,3,128,128]{4,3,2,1,0:T(8,128)(2,1)S(1)} %copy-done.18, bf16[16,258,1,128]{3,0,2,1:T(8,128)(2,1)S(1)} %collective-permute-done.11, ...), kind=kOutput, calls=%fused_computation.27 | convolution fusion | flops 9709973504 | bytes 19268096 | tf_op jit(solution)/shard_map/conv_general_dilated | solution.py:29
  370.4 22.4 %psum.52 = f32[16,32,2]{0,1,2:T(8,128)S(1)} all-reduce(f32[16,32,2]{0,1,2:T(8,128)S(1)} %pad_maximum_fusion.24), channel_id=1, replica_groups=mesh['dp'=1,'sx'=2,'sy'=4] {'sy','sx'}, use_global_device_ids=true, to_apply=%region_19.20 | all-reduce | flops 1024 | bytes 8192 | tf_op jit(solution)/shard_map/psum | solution.py:37
  393.1 7.8 fusion.33
  403.5 4.3 collective-permute-done.13
  412.6 20.7 %collective-permute-done.14 = bf16[16,258,1,128]{3,0,2,1:T(8,128)(2,1)S(1)} collective-permute-done((bf16[16,258,1,128]{3,0,2,1:T(8,128)(2,1)S(1)}, bf16[16,258,1,128]{3,0,2,1:T(8,128)(2,1)S(1)}, u32[]{:S(2)}, u32[]{:S(2)}) %collective-permute-start.14) | collective-permute-done | bytes 1056800 | tf_op jit(solution)/shard_map/ppermute | solution.py:24
  433.3 4.8 collective-permute-done.15
  438.1 22.8 %convert_reduce_fusion.1 = (f32[16,128]{1,0:T(8,128)S(1)}, f32[16,128]{1,0:T(8,128)S(1)}, bf16[16,256,8,128]{3,0,2,1:T(8,128)(2,1)}) fusion(bf16[16,256,8,128]{3,0,2,1:T(8,128)(2,1)S(1)} %bitcast.215, f32[128]{0:T(128)S(1)} %copy-done.17, bf16[5,3,3,128,128]{4,3,2,1,0:T(8,128)(2,1)S(1)} %copy-done.18, ...), kind=kOutput, calls=%fused_computation.14 | convolution fusion | flops 9718362112 | bytes 27656704 | tf_op jit(solution)/shard_map/conv_general_dilated | solution.py:29
  461.2 22.4 %psum.53 = f32[16,32,2]{0,1,2:T(8,128)S(1)} all-reduce(f32[16,32,2]{0,1,2:T(8,128)S(1)} %pad_maximum_fusion.25), channel_id=1, replica_groups=mesh['dp'=1,'sx'=2,'sy'=4] {'sy','sx'}, use_global_device_ids=true, to_apply=%region_24.25 | all-reduce | flops 1024 | bytes 8192 | tf_op jit(solution)/shard_map/psum | solution.py:37
  483.9 7.0 fusion.66
  493.5 4.3 collective-permute-done.17
  498.1 3.2 collective-permute-start.18
  502.6 20.7 %collective-permute-done.18 = bf16[16,258,1,128]{3,0,2,1:T(8,128)(2,1)S(1)} collective-permute-done((bf16[16,258,1,128]{3,0,2,1:T(8,128)(2,1)S(1)}, bf16[16,258,1,128]{3,0,2,1:T(8,128)(2,1)S(1)}, u32[]{:S(2)}, u32[]{:S(2)}) %collective-permute-start.18) | collective-permute-done | bytes 1056800 | tf_op jit(solution)/shard_map/ppermute | solution.py:24
  523.3 4.8 collective-permute-done.19
  528.0 22.2 %convert_reduce_fusion.4 = (f32[16,128]{1,0:T(8,128)S(1)}, f32[16,128]{1,0:T(8,128)S(1)}, bf16[16,256,8,128]{3,0,2,1:T(8,128)(2,1)}) fusion(f32[128]{0:T(128)S(1)} %copy-done.16, bf16[5,3,3,128,128]{4,3,2,1,0:T(8,128)(2,1)S(1)} %copy-done.18, bf16[16,258,1,128]{3,0,2,1:T(8,128)(2,1)S(1)} %collective-permute-done.19, ...), kind=kOutput, calls=%fused_computation.24 | convolution fusion | flops 9709973504 | bytes 19268096 | tf_op jit(solution)/shard_map/conv_general_dilated | solution.py:29
  550.6 22.4 %psum.54 = f32[16,32,2]{0,1,2:T(8,128)S(1)} all-reduce(f32[16,32,2]{0,1,2:T(8,128)S(1)} %pad_maximum_fusion.26), channel_id=1, replica_groups=mesh['dp'=1,'sx'=2,'sy'=4] {'sy','sx'}, use_global_device_ids=true, to_apply=%region_29.30 | all-reduce | flops 1024 | bytes 8192 | tf_op jit(solution)/shard_map/psum | solution.py:37
  573.3 7.8 fusion.41
  583.7 4.3 collective-permute-done.21
  588.2 3.2 collective-permute-start.22
  592.8 20.7 %collective-permute-done.22 = bf16[16,258,1,128]{3,0,2,1:T(8,128)(2,1)S(1)} collective-permute-done((bf16[16,258,1,128]{3,0,2,1:T(8,128)(2,1)S(1)}, bf16[16,258,1,128]{3,0,2,1:T(8,128)(2,1)S(1)}, u32[]{:S(2)}, u32[]{:S(2)}) %collective-permute-start.22) | collective-permute-done | bytes 1056800 | tf_op jit(solution)/shard_map/ppermute | solution.py:24
  613.5 4.8 collective-permute-done.23
  618.3 22.8 %convert_reduce_fusion.3 = (f32[16,128]{1,0:T(8,128)S(1)}, f32[16,128]{1,0:T(8,128)S(1)}, bf16[16,256,8,128]{3,0,2,1:T(8,128)(2,1)}) fusion(bf16[16,256,8,128]{3,0,2,1:T(8,128)(2,1)S(1)} %bitcast.217, f32[128]{0:T(128)S(1)} %copy-done.15, bf16[5,3,3,128,128]{4,3,2,1,0:T(8,128)(2,1)S(1)} %copy-done.18, ...), kind=kOutput, calls=%fused_computation.21 | convolution fusion | flops 9718362112 | bytes 27656704 | tf_op jit(solution)/shard_map/conv_general_dilated | solution.py:29
  641.3 22.4 %psum.55 = f32[16,32,2]{0,1,2:T(8,128)S(1)} all-reduce(f32[16,32,2]{0,1,2:T(8,128)S(1)} %pad_maximum_fusion.27), channel_id=1, replica_groups=mesh['dp'=1,'sx'=2,'sy'=4] {'sy','sx'}, use_global_device_ids=true, to_apply=%region_34.35 | all-reduce | flops 1024 | bytes 8192 | tf_op jit(solution)/shard_map/psum | solution.py:37
  664.0 7.0 fusion.49
  673.6 4.3 collective-permute-done.25
  682.7 20.6 %collective-permute-done.26 = bf16[16,258,1,128]{3,0,2,1:T(8,128)(2,1)S(1)} collective-permute-done((bf16[16,258,1,128]{3,0,2,1:T(8,128)(2,1)S(1)}, bf16[16,258,1,128]{3,0,2,1:T(8,128)(2,1)S(1)}, u32[]{:S(2)}, u32[]{:S(2)}) %collective-permute-start.26) | collective-permute-done | bytes 1056800 | tf_op jit(solution)/shard_map/ppermute | solution.py:24
  703.4 4.8 collective-permute-done.27
  708.2 99.1 %broadcast_add_fusion = f32[16,256,8,3]{0,3,2,1:T(4,128)} fusion(f32[3]{0:T(128)S(1)} %convert_element_type.251, bf16[3,3,128,3]{2,3,1,0:T(4,128)(2,1)S(1)} %copy-done.19, bf16[16,258,1,128]{3,0,2,1:T(8,128)(2,1)S(1)} %collective-permute-done.27, bf16[16,1,8,128]{3,0,2,1:T(8,128)(2,1)S(1)} %collective-permute-done.25, ...), kind=kOutput, calls=%fused_computation.160 | convolution fusion | flops 247726080 | bytes 10967820 | tf_op jit(solution)/shard_map/conv_general_dilated | solution.py:29
  807.2 3.9 copy.95
  (187 shorter events, 43.8 us)
Async XLA Ops:
  0.0 145.5 %copy-start = (bf16[3,3,256,128]{3,2,1,0:T(8,128)(2,1)S(1)}, bf16[3,3,256,128]{3,2,1,0:T(8,128)(2,1)}, u32[]{:S(2)}) copy-start(bf16[3,3,256,128]{3,2,1,0:T(8,128)(2,1)} %param.11) | copy-start | bytes 1769476
  0.0 55.3 %copy-start.5 = (bf16[2,256]{1,0:T(2,128)(2,1)S(1)}, bf16[2,256]{1,0:T(2,128)(2,1)}, u32[]{:S(2)}) copy-start(bf16[2,256]{1,0:T(2,128)(2,1)} %param.10) | copy-start | bytes 3076
  86.3 2.6 collective-permute-start
  87.6 5.6 collective-permute-start.1
  93.8 46.8 %collective-permute-start.2 = (bf16[16,258,1,256]{3,0,2,1:T(8,128)(2,1)S(1)}, bf16[16,258,1,256]{3,0,2,1:T(8,128)(2,1)S(1)}, u32[]{:S(2)}, u32[]{:S(2)}) collective-permute-start(bf16[16,258,1,256]{3,0,2,1:T(8,128)(2,1)S(1)} %get-tuple-element.33), channel_id=1, source_target_pairs={{0,4},{1,5},{2,6},{3,7}} | collective-permute-start | bytes 6340616 | tf_op jit(solution)/shard_map/ppermute | solution.py:24
  96.4 49.1 %collective-permute-start.3 = (bf16[16,258,1,256]{3,0,2,1:T(8,128)(2,1)S(1)}, bf16[16,258,1,256]{3,0,2,1:T(8,128)(2,1)S(1)}, u32[]{:S(2)}, u32[]{:S(2)}) collective-permute-start(bf16[16,258,1,256]{3,0,2,1:T(8,128)(2,1)S(1)} %get-tuple-element.34), channel_id=1, source_target_pairs={{4,0},{5,1},{6,2},{7,3}} | collective-permute-start | bytes 6340616 | tf_op jit(solution)/shard_map/ppermute | solution.py:25
  217.8 2.6 collective-permute-start.4
  219.1 5.6 collective-permute-start.5
  224.9 26.7 %collective-permute-start.6 = (bf16[16,258,1,128]{3,0,2,1:T(8,128)(2,1)S(1)}, bf16[16,258,1,128]{3,0,2,1:T(8,128)(2,1)S(1)}, u32[]{:S(2)}, u32[]{:S(2)}) collective-permute-start(bf16[16,258,1,128]{3,0,2,1:T(8,128)(2,1)S(1)} %get-tuple-element.47), channel_id=1, source_target_pairs={{0,4},{1,5},{2,6},{3,7}} | collective-permute-start | bytes 3170312 | tf_op jit(solution)/shard_map/ppermute | solution.py:24
  228.4 26.9 %copy-start.18 = (bf16[5,3,3,128,128]{4,3,2,1,0:T(8,128)(2,1)S(1)}, bf16[5,3,3,128,128]{4,3,2,1,0:T(8,128)(2,1)}, u32[]{:S(2)}) copy-start(bf16[5,3,3,128,128]{4,3,2,1,0:T(8,128)(2,1)} %param.14) | copy-start | bytes 4423684
  228.5 26.9 %collective-permute-start.7 = (bf16[16,258,1,128]{3,0,2,1:T(8,128)(2,1)S(1)}, bf16[16,258,1,128]{3,0,2,1:T(8,128)(2,1)S(1)}, u32[]{:S(2)}, u32[]{:S(2)}) collective-permute-start(bf16[16,258,1,128]{3,0,2,1:T(8,128)(2,1)S(1)} %get-tuple-element.48), channel_id=1, source_target_pairs={{4,0},{5,1},{6,2},{7,3}} | collective-permute-start | bytes 3170312 | tf_op jit(solution)/shard_map/ppermute | solution.py:25
  311.0 2.6 collective-permute-start.8
  312.3 5.6 collective-permute-start.9
  318.2 25.2 %collective-permute-start.10 = (bf16[16,258,1,128]{3,0,2,1:T(8,128)(2,1)S(1)}, bf16[16,258,1,128]{3,0,2,1:T(8,128)(2,1)S(1)}, u32[]{:S(2)}, u32[]{:S(2)}) collective-permute-start(bf16[16,258,1,128]{3,0,2,1:T(8,128)(2,1)S(1)} %get-tuple-element.45), channel_id=1, source_target_pairs={{0,4},{1,5},{2,6},{3,7}} | collective-permute-start | bytes 3170312 | tf_op jit(solution)/shard_map/ppermute | solution.py:24
  321.4 26.7 %collective-permute-start.11 = (bf16[16,258,1,128]{3,0,2,1:T(8,128)(2,1)S(1)}, bf16[16,258,1,128]{3,0,2,1:T(8,128)(2,1)S(1)}, u32[]{:S(2)}, u32[]{:S(2)}) collective-permute-start(bf16[16,258,1,128]{3,0,2,1:T(8,128)(2,1)S(1)} %get-tuple-element.46), channel_id=1, source_target_pairs={{4,0},{5,1},{6,2},{7,3}} | collective-permute-start | bytes 3170312 | tf_op jit(solution)/shard_map/ppermute | solution.py:25
  348.1 44.9 %copy-start.12 = (f32[128]{0:T(128)S(1)}, f32[128]{0:T(128)}, u32[]{:S(2)}) copy-start(f32[128]{0:T(128)} %get-tuple-element.73) | copy-start | bytes 1540
  348.2 44.9 %copy-start.13 = (f32[128]{0:T(128)S(1)}, f32[128]{0:T(128)}, u32[]{:S(2)}) copy-start(f32[128]{0:T(128)} %get-tuple-element.74) | copy-start | bytes 1540
  393.1 45.0 %slice-start = ((s8[8388608]{0:T(1024)(128)(4,1)}), s8[4194304]{0:T(1024)(128)(4,1)S(1)}, s32[]{:S(2)}) async-start(s8[8388608]{0:T(1024)(128)(4,1)} %bitcast.214), calls=%async_computation | async-start | bytes 8388608
  393.1 45.0 %slice-start.1 = ((s8[8388608]{0:T(1024)(128)(4,1)}), s8[4194304]{0:T(1024)(128)(4,1)S(1)}, s32[]{:S(2)}) async-start(s8[8388608]{0:T(1024)(128)(4,1)} %bitcast.214), calls=%async_computation.1 | async-start | bytes 8388608
  393.1 44.9 %copy-start.17 = (f32[128]{0:T(128)S(1)}, f32[128]{0:T(128)}, u32[]{:S(2)}) copy-start(f32[128]{0:T(128)} %get-tuple-element.63) | copy-start | bytes 1540
  400.9 2.6 collective-permute-start.12
  402.2 5.6 collective-permute-start.13
  408.1 25.2 %collective-permute-start.14 = (bf16[16,258,1,128]{3,0,2,1:T(8,128)(2,1)S(1)}, bf16[16,258,1,128]{3,0,2,1:T(8,128)(2,1)S(1)}, u32[]{:S(2)}, u32[]{:S(2)}) collective-permute-start(bf16[16,258,1,128]{3,0,2,1:T(8,128)(2,1)S(1)} %get-tuple-element.43), channel_id=1, source_target_pairs={{0,4},{1,5},{2,6},{3,7}} | collective-permute-start | bytes 3170312 | tf_op jit(solution)/shard_map/ppermute | solution.py:24
  411.3 26.7 %collective-permute-start.15 = (bf16[16,258,1,128]{3,0,2,1:T(8,128)(2,1)S(1)}, bf16[16,258,1,128]{3,0,2,1:T(8,128)(2,1)S(1)}, u32[]{:S(2)}, u32[]{:S(2)}) collective-permute-start(bf16[16,258,1,128]{3,0,2,1:T(8,128)(2,1)S(1)} %get-tuple-element.44), channel_id=1, source_target_pairs={{4,0},{5,1},{6,2},{7,3}} | collective-permute-start | bytes 3170312 | tf_op jit(solution)/shard_map/ppermute | solution.py:25
  438.1 45.8 %copy-start.10 = (f32[128]{0:T(128)S(1)}, f32[128]{0:T(128)}, u32[]{:S(2)}) copy-start(f32[128]{0:T(128)} %get-tuple-element.71) | copy-start | bytes 1540
  438.1 45.8 %copy-start.11 = (f32[128]{0:T(128)S(1)}, f32[128]{0:T(128)}, u32[]{:S(2)}) copy-start(f32[128]{0:T(128)} %get-tuple-element.72) | copy-start | bytes 1540
  483.9 44.2 %copy-start.16 = (f32[128]{0:T(128)S(1)}, f32[128]{0:T(128)}, u32[]{:S(2)}) copy-start(f32[128]{0:T(128)} %get-tuple-element.62) | copy-start | bytes 1540
  490.9 2.6 collective-permute-start.16
  492.2 5.6 collective-permute-start.17
  498.1 25.2 %collective-permute-start.18 = (bf16[16,258,1,128]{3,0,2,1:T(8,128)(2,1)S(1)}, bf16[16,258,1,128]{3,0,2,1:T(8,128)(2,1)S(1)}, u32[]{:S(2)}, u32[]{:S(2)}) collective-permute-start(bf16[16,258,1,128]{3,0,2,1:T(8,128)(2,1)S(1)} %get-tuple-element.41), channel_id=1, source_target_pairs={{0,4},{1,5},{2,6},{3,7}} | collective-permute-start | bytes 3170312 | tf_op jit(solution)/shard_map/ppermute | solution.py:24
  501.3 26.7 %collective-permute-start.19 = (bf16[16,258,1,128]{3,0,2,1:T(8,128)(2,1)S(1)}, bf16[16,258,1,128]{3,0,2,1:T(8,128)(2,1)S(1)}, u32[]{:S(2)}, u32[]{:S(2)}) collective-permute-start(bf16[16,258,1,128]{3,0,2,1:T(8,128)(2,1)S(1)} %get-tuple-element.42), channel_id=1, source_target_pairs={{4,0},{5,1},{6,2},{7,3}} | collective-permute-start | bytes 3170312 | tf_op jit(solution)/shard_map/ppermute | solution.py:25
  528.0 45.2 %copy-start.8 = (f32[128]{0:T(128)S(1)}, f32[128]{0:T(128)}, u32[]{:S(2)}) copy-start(f32[128]{0:T(128)} %get-tuple-element.69) | copy-start | bytes 1540
  528.0 45.2 %copy-start.9 = (f32[128]{0:T(128)S(1)}, f32[128]{0:T(128)}, u32[]{:S(2)}) copy-start(f32[128]{0:T(128)} %get-tuple-element.70) | copy-start | bytes 1540
  573.2 45.0 %slice-start.2 = ((s8[8388608]{0:T(1024)(128)(4,1)}), s8[4194304]{0:T(1024)(128)(4,1)S(1)}, s32[]{:S(2)}) async-start(s8[8388608]{0:T(1024)(128)(4,1)} %bitcast.216), calls=%async_computation.2 | async-start | bytes 8388608
  573.2 45.0 %slice-start.3 = ((s8[8388608]{0:T(1024)(128)(4,1)}), s8[4194304]{0:T(1024)(128)(4,1)S(1)}, s32[]{:S(2)}) async-start(s8[8388608]{0:T(1024)(128)(4,1)} %bitcast.216), calls=%async_computation.3 | async-start | bytes 8388608
  573.3 45.0 %copy-start.15 = (f32[128]{0:T(128)S(1)}, f32[128]{0:T(128)}, u32[]{:S(2)}) copy-start(f32[128]{0:T(128)} %get-tuple-element.61) | copy-start | bytes 1540
  581.1 2.6 collective-permute-start.20
  582.4 5.6 collective-permute-start.21
  588.2 25.2 %collective-permute-start.22 = (bf16[16,258,1,128]{3,0,2,1:T(8,128)(2,1)S(1)}, bf16[16,258,1,128]{3,0,2,1:T(8,128)(2,1)S(1)}, u32[]{:S(2)}, u32[]{:S(2)}) collective-permute-start(bf16[16,258,1,128]{3,0,2,1:T(8,128)(2,1)S(1)} %get-tuple-element.39), channel_id=1, source_target_pairs={{0,4},{1,5},{2,6},{3,7}} | collective-permute-start | bytes 3170312 | tf_op jit(solution)/shard_map/ppermute | solution.py:24
  591.5 26.7 %collective-permute-start.23 = (bf16[16,258,1,128]{3,0,2,1:T(8,128)(2,1)S(1)}, bf16[16,258,1,128]{3,0,2,1:T(8,128)(2,1)S(1)}, u32[]{:S(2)}, u32[]{:S(2)}) collective-permute-start(bf16[16,258,1,128]{3,0,2,1:T(8,128)(2,1)S(1)} %get-tuple-element.40), channel_id=1, source_target_pairs={{4,0},{5,1},{6,2},{7,3}} | collective-permute-start | bytes 3170312 | tf_op jit(solution)/shard_map/ppermute | solution.py:25
  618.2 45.7 %copy-start.6 = (f32[128]{0:T(128)S(1)}, f32[128]{0:T(128)}, u32[]{:S(2)}) copy-start(f32[128]{0:T(128)} %get-tuple-element.68) | copy-start | bytes 1540
  618.2 45.7 %copy-start.7 = (f32[128]{0:T(128)S(1)}, f32[128]{0:T(128)}, u32[]{:S(2)}) copy-start(f32[128]{0:T(128)} %get-tuple-element.79) | copy-start | bytes 1540
  664.0 44.2 %copy-start.19 = (bf16[3,3,128,3]{2,3,1,0:T(4,128)(2,1)S(1)}, bf16[3,3,128,3]{2,3,1,0:T(4,128)(2,1)}, u32[]{:S(2)}) copy-start(bf16[3,3,128,3]{2,3,1,0:T(4,128)(2,1)} %param.16) | copy-start | bytes 20740
  671.0 2.6 collective-permute-start.24
  672.3 5.6 collective-permute-start.25
  678.2 25.2 %collective-permute-start.26 = (bf16[16,258,1,128]{3,0,2,1:T(8,128)(2,1)S(1)}, bf16[16,258,1,128]{3,0,2,1:T(8,128)(2,1)S(1)}, u32[]{:S(2)}, u32[]{:S(2)}) collective-permute-start(bf16[16,258,1,128]{3,0,2,1:T(8,128)(2,1)S(1)} %get-tuple-element.37), channel_id=1, source_target_pairs={{0,4},{1,5},{2,6},{3,7}} | collective-permute-start | bytes 3170312 | tf_op jit(solution)/shard_map/ppermute | solution.py:24
  681.4 26.7 %collective-permute-start.27 = (bf16[16,258,1,128]{3,0,2,1:T(8,128)(2,1)S(1)}, bf16[16,258,1,128]{3,0,2,1:T(8,128)(2,1)S(1)}, u32[]{:S(2)}, u32[]{:S(2)}) collective-permute-start(bf16[16,258,1,128]{3,0,2,1:T(8,128)(2,1)S(1)} %get-tuple-element.38), channel_id=1, source_target_pairs={{4,0},{5,1},{6,2},{7,3}} | collective-permute-start | bytes 3170312 | tf_op jit(solution)/shard_map/ppermute | solution.py:25
  708.2 103.0 %copy-start.1 = (bf16[3,3,256,128]{3,2,1,0:T(8,128)(2,1)S(1)}, bf16[3,3,256,128]{3,2,1,0:T(8,128)(2,1)}, u32[]{:S(2)}) copy-start(bf16[3,3,256,128]{3,2,1,0:T(8,128)(2,1)} %param.11) | copy-start | bytes 1769476
  (5 other events, 66.0 us)
where the time goes:
time: 820 us; the launch traced here: 812 us
  matrix products  278 us (34%)
  waiting for transfers between devices  207 us (25%)
  blocking collectives  160 us (20%)
  other arithmetic  108 us (13%)
  starting transfers between devices  50.2 us (6%)
    conv_general_dilated x7, matrix products, conv_tile(): lax.conv_general_dilated(add_border(act_map), kernel, (1, 1), ((0, 0), (0...  257 us
    psum x7, blocking collectives, group_norm_act(): totals = lax.psum(jnp.stack([sum_one, sum_two], axis=-1), ('sy', 'sx'))  160 us
    ppermute x7, waiting for transfers between devices, add_border(): left_col = lax.ppermute(tall[:, :, -1:], 'sx', to_right)  145 us
    convert_element_type x7, other arithmetic, group_norm_act(): jax.nn.silu(act_map.astype(jnp.float32) * chan_scale[:, None, None, :] +...  74.5 us
    ppermute x7, waiting for transfers between devices, add_border(): right_col = lax.ppermute(tall[:, :, :1], 'sx', to_left)  32.3 us
    ppermute x7, waiting for transfers between devices, add_border(): bottom_row = lax.ppermute(act_map[:, :1], 'sy', to_above)  30 us
    reduce_sum x8, other arithmetic, group_norm_act(): jnp.sum(act_map, axis=(1, 2), dtype=jnp.float32)  29.9 us
    ppermute x7, starting transfers between devices, add_border(): left_col = lax.ppermute(tall[:, :, -1:], 'sx', to_right)  22.3 us
  transfers between devices with their start and end apart: 28, of which 20 were waited for; matrix products, arithmetic and copies ran while one was open for 3% of the time, Pallas kernels for 0%

commit v1 on v0

v1 whole, which is shorter than its diff:
```python
import jax
import jax.numpy as jnp
from jax import lax
from jax.experimental import pallas as pl
from jax.experimental.pallas import tpu as pltpu
from jax.sharding import PartitionSpec as P

MESH = pl.DeviceIdType.MESH
GN_EPS = 1e-6
NG = 4
NS = 4
SUB = 16
J = 8
BC = 8
RC = 8
RB = 4
LAYERS = 7


def solution(mesh):
    tile_spec = P("dp", "sy", "sx", None)
    rep = P()

    def kernel(a_hbm, w1_ref, wr_ref, ws_ref, wo_ref, nrm_ref, bias_ref, y_ref,
               a_buf, t_buf, h_buf, cola, colx, rowa, rowx, cora, corx, act, wp1, wp2, wpr, wpo,
               raw, tmp, sacc, stat_own, stat_in, sb,
               raw_sem, col_s, col_r, row_s, row_r, cor_s, cor_r, st_s, st_r):
        sx = lax.axis_index("sx")
        sy = lax.axis_index("sy")
        px = 1 - sx
        up = lax.rem(sy + 3, 4)
        dn = lax.rem(sy + 1, 4)
        me = sx * 4 + sy
        R = a_buf.shape[1]
        count = 1024.0 * 16.0

        def peer(d):
            other = lax.rem(me + d, 8)
            return {"sx": lax.div(other, 4), "sy": lax.rem(other, 4)}

        barrier = pltpu.get_barrier_semaphore()
        for d in range(1, 8):
            pl.semaphore_signal(barrier, inc=1, device_id=peer(d), device_id_type=MESH)

        def raw_copy(g, chunk, slot):
            return pltpu.make_async_copy(
                a_hbm.at[pl.ds(g * NS, NS), :, pl.ds(chunk * RC, RC)], raw.at[slot], raw_sem.at[slot])

        nchunk = R // RC
        raw_copy(0, 0, 0).start()

        def rcopy(src, dst, ss, rs, dev):
            return pltpu.make_async_remote_copy(src_ref=src, dst_ref=dst, send_sem=ss, recv_sem=rs, device_id=dev, device_id_type=MESH)

        def xbuf(l):
            return a_buf if l == 0 else (t_buf if l % 2 else h_buf)

        def halo_copies(l, g):
            x = xbuf(l)
            if l == 0:
                col, row, cor = cola.at[g], rowa.at[g], cora.at[g]
            else:
                col, row, cor = colx.at[l % 2, g], rowx.at[l % 2, g], corx.at[l % 2, g]
            return [
                rcopy(x.at[g, R - 1], row.at[0], row_s.at[l, g, 0], row_r.at[l, g, 0], {"sx": sx, "sy": dn}),
                rcopy(x.at[g, 0], row.at[1], row_s.at[l, g, 1], row_r.at[l, g, 1], {"sx": sx, "sy": up}),
                rcopy(x.at[g, R - 1, 0], cor.at[0], cor_s.at[l, g, 0], cor_r.at[l, g, 0], {"sx": px, "sy": dn}),
                rcopy(x.at[g, 0, 0], cor.at[1], cor_s.at[l, g, 1], cor_r.at[l, g, 1], {"sx": px, "sy": up}),
                rcopy(x.at[g, :, 0], col, col_s.at[l, g], col_r.at[l, g], {"sx": px, "sy": sy}),
            ]

        def stat_copies(l, g):
            nh = 2 if l == 0 else 1
            return [
                rcopy(stat_own.at[l % 2, g, pl.ds(0, nh)], stat_in.at[l % 2, g, d - 1, pl.ds(0, nh)],
                      st_s.at[l, g, d - 1], st_r.at[l, g, d - 1], peer(d))
                for d in range(1, 8)
            ]

        sub8 = lax.broadcasted_iota(jnp.int32, (8, 128), 0)
        lane8 = lax.broadcasted_iota(jnp.int32, (8, 128), 1)

        def fold(v):
            v = v[0:8] + v[8:16]
            return v + pltpu.roll(v, 4, 0)

        def push_stats(l, g):
            for half in range(2 if l == 0 else 1):
                one = fold(sacc[0, half])
                two = fold(sacc[1, half])
                stat_own[l % 2, g, half] = jnp.where(sub8 < 4, one, two)
            for c in stat_copies(l, g):
                c.start()

        def zero_stats():
            sacc[...] = jnp.zeros_like(sacc)

        def load_group(g, _):
            zero_stats()

            def load_chunk(ch, _):
                step = g * nchunk + ch
                slot = lax.rem(step, 2)
                nxt = step + 1

                @pl.when(nxt < NG * nchunk)
                def _():
                    raw_copy(lax.div(nxt, nchunk), lax.rem(nxt, nchunk), lax.rem(nxt, 2)).start()

                raw_copy(g, ch, slot).wait()
                ones = [jnp.zeros((SUB, 128), jnp.float32) for _ in range(2)]
                twos = [jnp.zeros((SUB, 128), jnp.float32) for _ in range(2)]
                for r in range(RC):
                    for p in range(NG):
                        for i in range(NS):
                            v = raw[slot, i, p, r].astype(jnp.float32)
                            base = (p * NS + i) * J
                            tmp[r % 2, 0, base:base + J, :] = v[:, :128]
                            tmp[r % 2, 1, base:base + J, :] = v[:, 128:]
                    for w in range(J):
                        j = sx * w + (1 - sx) * (J - 1 - w)
                        for half in range(2):
                            v = tmp[r % 2, half, pl.ds(w, SUB, stride=J), :]
                            a_buf[g, ch * RC + r, j, :, half * 128:(half + 1) * 128] = v.astype(jnp.bfloat16)
                            ones[half] = ones[half] + v
                            twos[half] = twos[half] + v * v
                for half in range(2):
                    sacc[0, half] = sacc[0, half] + ones[half]
                    sacc[1, half] = sacc[1, half] + twos[half]
                return 0

            lax.fori_loop(0, nchunk, load_chunk, 0)

            @pl.when(g == 0)
            def _():
                pl.semaphore_wait(barrier, 7)

            push_stats(0, g)
            for c in halo_copies(0, g):
                c.start()
            return 0

        lax.fori_loop(0, NG, load_group, 0)

        def fill_pairs(dst, get, ch):
            zero = jnp.zeros((ch, 128), jnp.bfloat16)
            for dy in range(3):
                for d4 in range(4):
                    k = (dy * 4 + d4) * ch
                    dst[k:k + ch, 0:128] = get(dy, d4) if d4 < 3 else zero
                    dst[k:k + ch, 128:256] = get(dy, d4 - 1) if d4 > 0 else zero

        def real_dx(dx):
            return sx * dx + (1 - sx) * (2 - dx)

        fill_pairs(wp1, lambda dy, dx: w1_ref[dy, real_dx(dx)], 256)
        fill_pairs(wp2, lambda dy, dx: wr_ref[0, dy, real_dx(dx)], 128)
        zs = jnp.zeros((256, 128), jnp.bfloat16)
        wp2[1536:1792, 0:128] = ws_ref[...]
        wp2[1536:1792, 128:256] = zs
        wp2[1792:2048, 0:128] = zs
        wp2[1792:2048, 128:256] = ws_ref[...]
        for k in range(1, 5):
            fill_pairs(wpr.at[k - 1], lambda dy, dx, k=k: wr_ref[k, dy, real_dx(dx)], 128)

        lane128 = lax.broadcasted_iota(jnp.int32, (128, 128), 1)

        def fill_out(c, _):
            wpad = sx * c + (1 - sx) * (J + 1 - c)
            placed = []
            for dy in range(3):
                rolled = pltpu.roll(wo_ref[dy], lax.rem(3 * wpad - 6 + 128, 128), 1)
                placed.append(jnp.where(lane128 < 3 * J, rolled, 0.0))
            for i in range(RB + 2):
                total = jnp.zeros((128, 128), jnp.float32)
                for dy in range(3):
                    ro = i - dy
                    if 0 <= ro < RB:
                        total = total + (pltpu.roll(placed[dy], 3 * J * ro, 1) if ro else placed[dy])
                wpo[i, c] = total.astype(jnp.bfloat16)
            return 0

        lax.fori_loop(0, J + 2, fill_out, 0)

        zc = jnp.zeros((R + 2, SUB, 256), jnp.bfloat16)
        act[:, J + 1] = zc

        sub16 = lax.broadcasted_iota(jnp.int32, (SUB, 128), 0)

        def scales(l, g):
            nh = 2 if l == 0 else 1
            per = 8 if l == 0 else 4
            for c in stat_copies(l, g):
                c.wait()
            for half in range(nh):
                x = stat_own[l % 2, g, half]
                for d in range(7):
                    x = x + stat_in[l % 2, g, d, half]
                k = 1
                while k < per:
                    x = x + jnp.where((lane8 & k) == 0, pltpu.roll(x, 128 - k, 1), pltpu.roll(x, k, 1))
                    k *= 2
                flip = pltpu.roll(x, 4, 0)
                mean = jnp.where(sub8 < 4, x, flip) / (count * per)
                var = jnp.where(sub8 < 4, flip, x) / (count * per) - mean * mean
                gain = nrm_ref[2 * l:2 * l + 1, half * 128:(half + 1) * 128]
                shift = nrm_ref[2 * l + 1:2 * l + 2, half * 128:(half + 1) * 128]
                s = lax.rsqrt(var + GN_EPS) * gain
                b = shift - mean * s
                sb[0, half] = 0.5 * jnp.concatenate([s, s], axis=0)
                sb[1, half] = 0.5 * jnp.concatenate([b, b], axis=0)

        def silu(x, half):
            u = x * sb[0, half] + sb[1, half]
            return u + u * jnp.tanh(u)

        def activate(l, g):
            nh = 2 if l == 0 else 1
            x = xbuf(l)

            def row(r, _):
                for j in range(J):
                    for half in range(nh):
                        sl = slice(half * 128, half * 128 + 128)
                        act[r + 1, j + 1, :, sl] = silu(x[g, r, j, :, sl].astype(jnp.float32), half).astype(jnp.bfloat16)
                return 0

            lax.fori_loop(0, R, row, 0)
            for c in halo_copies(l, g):
                c.wait()
            if l == 0:
                col, rw, cor = cola.at[g], rowa.at[g], cora.at[g]
            else:
                col, rw, cor = colx.at[l % 2, g], rowx.at[l % 2, g], corx.at[l % 2, g]

            def colrow(q, _):
                for k in range(8):
                    r = q * 8 + k
                    for half in range(nh):
                        sl = slice(half * 128, half * 128 + 128)
                        act[r + 1, 0, :, sl] = silu(col[r, :, sl].astype(jnp.float32), half).astype(jnp.bfloat16)
                return 0

            lax.fori_loop(0, R // 8, colrow, 0)
            for side in range(2):
                shift = NS if side == 0 else SUB - NS
                outer = (sub16 < NS) if side == 0 else (sub16 >= SUB - NS)
                border = jnp.logical_and(outer, sy == (0 if side == 0 else 3))
                own_row = R - 1 if side == 0 else 0
                for j in range(-1, J):
                    for half in range(nh):
                        sl = slice(half * 128, half * 128 + 128)
                        if j < 0:
                            own, far = col[own_row, :, sl], cor[side, :, sl]
                        else:
                            own, far = x[g, own_row, j, :, sl], rw[side, j, :, sl]
                        own = pltpu.roll(own.astype(jnp.float32), shift, 0)
                        far = pltpu.roll(far.astype(jnp.float32), shift, 0)
                        v = silu(jnp.where(outer, far, own), half)
                        v = jnp.where(border, 0.0, v)
                        act[0 if side == 0 else R + 1, j + 1, :, sl] = v.astype(jnp.bfloat16)

        def conv(l, g):
            ch = 256 if l == 0 else 128
            wp = wp1 if l == 0 else (wp2 if l == 1 else wpr.at[l - 2])
            out = xbuf(l + 1)
            if l == 1:
                bias = bias_ref[1:2] + bias_ref[6:7]
            else:
                bias = bias_ref[l:l + 1]
            bias = jnp.broadcast_to(bias.reshape(1, 1, 128), (BC, SUB, 128))

            def block(b, carry):
                one, two = carry
                r0 = b * BC
                rows = []
                for q in range(J // 2):
                    taps = []
                    for dy in range(3):
                        for d4 in range(4):
                            taps.append(act[pl.ds(r0 + dy, BC), 2 * q + d4, :, 0:ch].reshape(BC * SUB, ch))
                    if l == 1:
                        for s in range(2):
                            taps.append(a_buf[g, pl.ds(r0, BC), 2 * q + s].reshape(BC * SUB, 256))
                    rows.append(jnp.concatenate(taps, axis=1))
                lhs = jnp.concatenate(rows, axis=0)
                acc = jnp.dot(lhs, wp[...], preferred_element_type=jnp.float32)
                for q in range(J // 2):
                    for s in range(2):
                        v = acc[q * BC * SUB:(q + 1) * BC * SUB, s * 128:(s + 1) * 128].reshape(BC, SUB, 128) + bias
                        if l in (3, 5):
                            v = v + out[g, pl.ds(r0, BC), 2 * q + s].astype(jnp.float32)
                        v = v.astype(jnp.bfloat16)
                        out[g, pl.ds(r0, BC), 2 * q + s] = v
                        v = v.astype(jnp.float32)
                        one = one + jnp.sum(v, axis=0)
                        two = two + jnp.sum(v * v, axis=0)
                return one, two

            z = jnp.zeros((SUB, 128), jnp.float32)
            one, two = lax.fori_loop(0, R // BC, block, (z, z))
            sacc[0, 0] = one
            sacc[1, 0] = two

        def head(g):
            nb = R // RB
            taps = []
            for i in range(RB + 2):
                for c in range(J + 2):
                    parts = [act[RB * b + i, c, :, 0:128] for b in range(nb)]
                    taps.append(jnp.concatenate(parts, axis=0))
            acc = jnp.zeros((nb * SUB, 128), jnp.float32)
            for k in range(0, len(taps), 2):
                i, c = divmod(k, J + 2)
                w = wpo[i, pl.ds(c, 2)].reshape(256, 128)
                acc = acc + jnp.dot(jnp.concatenate(taps[k:k + 2], axis=1), w, preferred_element_type=jnp.float32)
            y_ref[g] = acc.reshape(nb, SUB, 128)

        for l in range(LAYERS):
            def phase(g, _, l=l):
                scales(l, g)
                activate(l, g)
                if l < LAYERS - 1:
                    conv(l, g)
                    push_stats(l + 1, g)
                    for c in halo_copies(l + 1, g):
                        c.start()
                else:
                    head(g)
                return 0

            lax.fori_loop(0, NG, phase, 0)

    def local_decode(act_in, norm_first, w_first, w_short, norm_rest, w_rest, bias_rest, w_out, bias_out):
        n, h, w, cin = act_in.shape
        rr = h // NG
        a = act_in.reshape(n, NG, rr, w, cin)
        f32 = jnp.float32
        nrm = jnp.concatenate([norm_first.astype(f32), jnp.pad(norm_rest.astype(f32).reshape(12, 128), ((0, 0), (0, 128)))], axis=0)
        nrm = jnp.pad(nrm, ((0, 2), (0, 0)))
        bias = jnp.pad(bias_rest.astype(f32), ((0, 1), (0, 0)))
        wo = jnp.transpose(w_out[:, ::-1], (0, 2, 1, 3)).reshape(3, 128, 9).astype(f32)
        wo = jnp.pad(wo, ((0, 0), (0, 0), (0, 119)))
        vm = pl.BlockSpec(memory_space=pltpu.VMEM)
        bf = jnp.bfloat16
        y = pl.pallas_call(
            kernel,
            out_shape=jax.ShapeDtypeStruct((NG, rr // RB, SUB, 128), f32),
            in_specs=[pl.BlockSpec(memory_space=pl.ANY)] + [vm] * 6,
            out_specs=vm,
            scratch_shapes=[
                pltpu.VMEM((NG, rr, J, SUB, 256), bf),
                pltpu.VMEM((NG, rr, J, SUB, 128), bf),
                pltpu.VMEM((NG, rr, J, SUB, 128), bf),
                pltpu.VMEM((NG, rr, SUB, 256), bf),
                pltpu.VMEM((2, NG, rr, SUB, 128), bf),
                pltpu.VMEM((NG, 2, J, SUB, 256), bf),
                pltpu.VMEM((2, NG, 2, J, SUB, 128), bf),
                pltpu.VMEM((NG, 2, SUB, 256), bf),
                pltpu.VMEM((2, NG, 2, SUB, 128), bf),
                pltpu.VMEM((rr + 2, J + 2, SUB, 256), bf),
                pltpu.VMEM((3072, 256), bf),
                pltpu.VMEM((2048, 256), bf),
                pltpu.VMEM((4, 1536, 256), bf),
                pltpu.VMEM((RB + 2, J + 2, 128, 128), bf),
                pltpu.VMEM((2, NS, NG, RC, J, 256), bf),
                pltpu.VMEM((2, 2, SUB * J, 128), f32),
                pltpu.VMEM((2, 2, SUB, 128), f32),
                pltpu.VMEM((2, NG, 2, 8, 128), f32),
                pltpu.VMEM((2, NG, 7, 2, 8, 128), f32),
                pltpu.VMEM((2, 2, SUB, 128), f32),
                pltpu.SemaphoreType.DMA((2,)),
                pltpu.SemaphoreType.DMA((LAYERS, NG)),
                pltpu.SemaphoreType.DMA((LAYERS, NG)),
                pltpu.SemaphoreType.DMA((LAYERS, NG, 2)),
                pltpu.SemaphoreType.DMA((LAYERS, NG, 2)),
                pltpu.SemaphoreType.DMA((LAYERS, NG, 2)),
                pltpu.SemaphoreType.DMA((LAYERS, NG, 2)),
                pltpu.SemaphoreType.DMA((LAYERS, NG, 7)),
                pltpu.SemaphoreType.DMA((LAYERS, NG, 7)),
            ],
            compiler_params=pltpu.CompilerParams(collective_id=0, has_side_effects=True, vmem_limit_bytes=67043328),
            name="decode",
        )(a, w_first, w_rest, w_short, wo, nrm, bias)
        y = y[..., :RB * J * 3].reshape(NG, rr // RB, NG, NS, RB, J, 3)
        y = jnp.transpose(y, (0, 3, 2, 1, 4, 5, 6)).reshape(n, h, w, 3)
        return y + bias_out.astype(f32)

    return jax.shard_map(local_decode, mesh=mesh, in_specs=(tile_spec,) + (rep,) * 8, out_specs=tile_spec, check_vma=False)
```

time: 820 us -> 254 us (0.31)
  matrix products: 278 us -> 0 us
  Pallas kernels: 0 us -> 228 us
  waiting for transfers between devices: 207 us -> 0 us
  blocking collectives: 160 us -> 0 us
  other arithmetic: 108 us -> 11 us
  starting transfers between devices: 50.2 us -> 0 us
    conv_general_dilated x7 -> x0, matrix products: 257 us -> none  [conv_tile(): lax.conv_general_dilated(add_border(act_map), kernel, (1, 1), ((0, 0), (0...]
    pallas_call x0 -> x1, Pallas kernels: none -> 228 us  [local_decode(): pl.pallas_call(kernel, out_shape=jax.ShapeDtypeStruct((NG, rr // RB, SUB,...]
    ppermute x28 -> x0, waiting for transfers between devices: 207 us -> none  [the longest x7 145 us: add_border(): left_col = lax.ppermute(tall[:, :, -1:], 'sx', to_right)]
    psum x7 -> x0, blocking collectives: 160 us -> none  [group_norm_act(): totals = lax.psum(jnp.stack([sum_one, sum_two], axis=-1), ('sy', 'sx'))]
    convert_element_type x10 -> x1, other arithmetic: 75.1 us -> 1.19 us  [local_decode(): return y + bias_out.astype(f32)]
    ppermute x28 -> x0, starting transfers between devices: 50.2 us -> none  [the longest x7 22.3 us: add_border(): left_col = lax.ppermute(tall[:, :, -1:], 'sx', to_right)]
    reduce_sum x15 -> x0, other arithmetic: 30.2 us -> none  [the longest x8 29.9 us: group_norm_act(): jnp.sum(act_map, axis=(1, 2), dtype=jnp.float32)]
    dot_general x1 -> x0, matrix products: 21.3 us -> none  [local_decode(): jnp.einsum('nhwc,cd->nhwd', act_in, w_short, preferred_element_type=jnp.f...]
  transfers between devices with their start and end apart: 28 -> 0, of which waited for: 20 -> 0; matrix products, arithmetic and copies ran while one was open for 3% -> 0% of each run, Pallas kernels for 0% -> 0%
where the time goes in v1:
time: 254 us; the launch traced here: 253 us
  Pallas kernels  228 us (90%)
  local copies, waits for them, and re-layouts  13.9 us (5%)
  other arithmetic  11 us (4%)
    pallas_call x1, Pallas kernels, local_decode(): pl.pallas_call(kernel, out_shape=jax.ShapeDtypeStruct((NG, rr // RB, SUB,...  228 us
    add x1, other arithmetic, local_decode(): return y + bias_out.astype(f32)  6.52 us
    add x1, local copies, waits for them, and re-layouts, local_decode(): return y + bias_out.astype(f32)  5.1 us

profile of v1, /device:TPU:0, one launch (start us, length us, event | category | flops | bytes accessed | tf_op | source)
XLA Modules:
  0.0 253.3 jit_solution(10719094837890112570)
XLA Ops:
  0.0 1.2 convert_element_type.23
  1.2 0.7 reshape.18
  1.9 0.7 fusion.1
  2.6 1.3 pad_convert_fusion.2.bias_ref
  3.9 0.6 pad_convert_fusion.1.nrm_ref
  4.5 0.7 reverse_bitcast_fusion
  5.2 0.1 copy.13
  5.3 0.7 pad_convert_fusion.wo_ref
  6.0 228.4 %decode.1 = f32[4,16,16,128]{3,2,1,0:T(8,128)} custom-call(bf16[16,4,64,8,256]{4,3,2,1,0:T(8,128)(2,1)} %bitcast.10, bf16[3,3,256,128]{3,2,1,0:T(8,128)(2,1)} %w1_ref.1, bf16[5,3,3,128,128]{4,3,2,1,0:T(8,128)(2,1)} %wr_ref.1, bf16[256,128]{1,0:T(8,128)(2,1)} %ws_ref.1, f32[3,128,128]{2,1,0:T(8,128)} %pad_convert_fusion.wo_ref, ...), custom_call_target="tpu_custom_call" | custom-call | tf_op jit(solution)/shard_map/decode/pallas_call | solution.py:346
  234.4 0.0 copy-start
  234.4 2.4 copy.14
  236.9 4.8 %copy.15 = f32[4,4,4,16,4,8,3]{5,4,3,2,6,1,0:T(4,128)} copy(f32[4,4,4,16,4,8,3]{3,1,2,6,5,4,0:T(4,128)S(1)} %bitcast.11) | data formatting | bytes 786432 | tf_op jit(solution)/shard_map/transpose | solution.py:386
  241.7 0.0 copy-done
  241.7 6.5 %broadcast_add_fusion = f32[16,256,8,3]{2,1,3,0:T(8,128)} fusion(f32[16,256,8,3]{2,1,3,0:T(8,128)} %bitcast.9, f32[3]{0:T(128)S(1)} %copy-done), kind=kLoop, calls=%fused_computation | loop fusion | flops 98304 | bytes 786444 | tf_op jit(solution)/shard_map/add | solution.py:387
  248.2 5.1 %copy.16 = f32[16,256,8,3]{1,2,3,0:T(8,128)} copy(f32[16,256,8,3]{2,1,3,0:T(8,128)} %broadcast_add_fusion) | data formatting | bytes 786432 | tf_op jit(solution)/shard_map/add | solution.py:387
  (1 shorter events, 0.0 us)
Async XLA Ops:
  234.4 7.2 %copy-start = (f32[3]{0:T(128)S(1)}, f32[3]{0:T(128)}, u32[]{:S(2)}) copy-start(f32[3]{0:T(128)} %convert_element_type.23) | copy-start | bytes 40

commit v2 on v0

v2 whole, which is shorter than its diff:
```python
import jax
import jax.numpy as jnp
from jax import lax
from jax.experimental import pallas as pl
from jax.experimental.pallas import tpu as pltpu
from jax.sharding import PartitionSpec as P

MESH = pl.DeviceIdType.MESH
GN_EPS = 1e-6
NG = 4
NS = 4
SUB = 16
J = 8
BC = 8
RC = 8
RB = 4
LAYERS = 7
CH = 128
CIN = 256
TAPS = 12


def solution(mesh):
    tile_spec = P("dp", "sy", "sx", None)
    rep = P()

    def kernel(a_hbm, w1_ref, wr_ref, ws_ref, wo_ref, n0_ref, nr_ref, bias_ref, bo_ref, y_ref,
               a_buf, t_buf, h_buf, rowa, rowx, cora, corx, act0, act1, act, wp1, wp2, wpr, wpo,
               raw, tmp, bias_rows, sacc, st_own, st_in, st_sum, st_far, sb,
               raw_sem, col_s, col_r, row_s, row_r, cor_s, cor_r, st_s, st_r, far_s, far_r):
        sx = lax.axis_index("sx")
        sy = lax.axis_index("sy")
        px = 1 - sx
        up = lax.rem(sy + 3, 4)
        dn = lax.rem(sy + 1, 4)
        R = a_buf.shape[1] - 2
        count = 1024.0 * 16.0
        f32, bf = jnp.float32, jnp.bfloat16

        barrier = pltpu.get_barrier_semaphore()
        friends = [{"sx": sx, "sy": lax.rem(sy + d, 4)} for d in range(1, 4)]
        friends += [{"sx": px, "sy": sy}, {"sx": px, "sy": up}, {"sx": px, "sy": dn}]
        for dev in friends:
            pl.semaphore_signal(barrier, inc=1, device_id=dev, device_id_type=MESH)

        def raw_copy(g, chunk, slot):
            return pltpu.make_async_copy(
                a_hbm.at[pl.ds(g * NS, NS), :, pl.ds(chunk * RC, RC)], raw.at[slot], raw_sem.at[slot])

        nchunk = R // RC
        raw_copy(0, 0, 0).start()

        def rcopy(src, dst, ss, rs, dev):
            return pltpu.make_async_remote_copy(src_ref=src, dst_ref=dst, send_sem=ss, recv_sem=rs, device_id=dev, device_id_type=MESH)

        def kind(l):
            return l if isinstance(l, int) else l[0]

        def index(l):
            return l if isinstance(l, int) else l[1]

        def after(l):
            return l + 1 if isinstance(l, int) else (5 - l[0], l[1] + 1)

        def halves(l):
            return 2 if kind(l) == 0 else 1

        def xbuf(l):
            return a_buf if kind(l) == 0 else (t_buf if kind(l) % 2 else h_buf)

        def halo_bufs(l, g):
            if kind(l) == 0:
                return rowa.at[g], cora.at[g]
            return rowx.at[kind(l) % 2, g], corx.at[kind(l) % 2, g]

        def halo_copies(l, g):
            x = xbuf(l)
            row, cor = halo_bufs(l, g)
            return [
                rcopy(x.at[g, R, pl.ds(1, J)], row.at[0], row_s.at[index(l), g, 0], row_r.at[index(l), g, 0], {"sx": sx, "sy": dn}),
                rcopy(x.at[g, 1, pl.ds(1, J)], row.at[1], row_s.at[index(l), g, 1], row_r.at[index(l), g, 1], {"sx": sx, "sy": up}),
                rcopy(x.at[g, R, 1], cor.at[0], cor_s.at[index(l), g, 0], cor_r.at[index(l), g, 0], {"sx": px, "sy": dn}),
                rcopy(x.at[g, 1, 1], cor.at[1], cor_s.at[index(l), g, 1], cor_r.at[index(l), g, 1], {"sx": px, "sy": up}),
                rcopy(x.at[g, pl.ds(1, R), 1], x.at[g, pl.ds(1, R), 0], col_s.at[index(l), g], col_r.at[index(l), g], {"sx": px, "sy": sy}),
            ]

        def near_copies(l, g):
            nh = halves(l)
            return [
                rcopy(st_own.at[kind(l) % 2, g, pl.ds(0, nh)], st_in.at[kind(l) % 2, g, d - 1, pl.ds(0, nh)],
                      st_s.at[index(l), g, d - 1], st_r.at[index(l), g, d - 1], friends[d - 1])
                for d in range(1, 4)
            ]

        def far_copy(l, g):
            nh = halves(l)
            return rcopy(st_sum.at[kind(l) % 2, g, pl.ds(0, nh)], st_far.at[kind(l) % 2, g, pl.ds(0, nh)],
                         far_s.at[index(l), g], far_r.at[index(l), g], {"sx": px, "sy": sy})

        sub8 = lax.broadcasted_iota(jnp.int32, (8, CH), 0)
        lane8 = lax.broadcasted_iota(jnp.int32, (8, CH), 1)
        sub16 = lax.broadcasted_iota(jnp.int32, (SUB, CH), 0)

        def fold(v):
            v = v[0:8] + v[8:16]
            return v + pltpu.roll(v, 4, 0)

        def push_sums(l, g):
            for half in range(halves(l)):
                st_own[kind(l) % 2, g, half] = jnp.where(sub8 < 4, fold(sacc[0, half]), fold(sacc[1, half]))
            for c in near_copies(l, g):
                c.start()

        def relay_sums(l, g):
            for c in near_copies(l, g):
                c.wait()
            for half in range(halves(l)):
                x = st_own[kind(l) % 2, g, half]
                for d in range(3):
                    x = x + st_in[kind(l) % 2, g, d, half]
                st_sum[kind(l) % 2, g, half] = x
            far_copy(l, g).start()

        def load_group(g, _):
            sacc[...] = jnp.zeros_like(sacc)

            def load_chunk(ch, _):
                step = g * nchunk + ch
                slot = lax.rem(step, 2)
                nxt = step + 1

                @pl.when(nxt < NG * nchunk)
                def _():
                    raw_copy(lax.div(nxt, nchunk), lax.rem(nxt, nchunk), lax.rem(nxt, 2)).start()

                raw_copy(g, ch, slot).wait()
                ones = [jnp.zeros((SUB, CH), f32) for _ in range(2)]
                twos = [jnp.zeros((SUB, CH), f32) for _ in range(2)]
                for r in range(RC):
                    for p in range(NG):
                        for i in range(NS):
                            v = raw[slot, i, p, r].astype(f32)
                            base = (p * NS + i) * J
                            tmp[r % 2, 0, base:base + J, :] = v[:, :CH]
                            tmp[r % 2, 1, base:base + J, :] = v[:, CH:]
                    for w in range(J):
                        j = sx * w + (1 - sx) * (J - 1 - w)
                        for half in range(2):
                            v = tmp[r % 2, half, pl.ds(w, SUB, stride=J), :]
                            a_buf[g, ch * RC + r + 1, j + 1, half] = v.astype(bf)
                            ones[half] = ones[half] + v
                            twos[half] = twos[half] + v * v
                for half in range(2):
                    sacc[0, half] = sacc[0, half] + ones[half]
                    sacc[1, half] = sacc[1, half] + twos[half]
                return 0

            lax.fori_loop(0, nchunk, load_chunk, 0)

            @pl.when(g == 0)
            def _():
                pl.semaphore_wait(barrier, len(friends))

            push_sums(0, g)

            @pl.when(g > 0)
            def _():
                relay_sums(0, g - 1)

            for c in halo_copies(0, g):
                c.start()
            return 0

        lax.fori_loop(0, NG, load_group, 0)

        def fill_pairs(dst, get, ch):
            zero = jnp.zeros((ch, CH), bf)
            for dy in range(3):
                for d4 in range(4):
                    k = (dy * 4 + d4) * ch
                    dst[k:k + ch, 0:CH] = get(dy, d4) if d4 < 3 else zero
                    dst[k:k + ch, CH:CIN] = get(dy, d4 - 1) if d4 > 0 else zero

        def real_dx(dx):
            return sx * dx + (1 - sx) * (2 - dx)

        fill_pairs(wp1, lambda dy, dx: w1_ref[dy, real_dx(dx)], CIN)
        relay_sums(0, NG - 1)
        fill_pairs(wp2, lambda dy, dx: wr_ref[0, dy, real_dx(dx)], CH)
        zs = jnp.zeros((CIN, CH), bf)
        wp2[1536:1792, 0:CH] = ws_ref[...]
        wp2[1536:1792, CH:CIN] = zs
        wp2[1792:2048, 0:CH] = zs
        wp2[1792:2048, CH:CIN] = ws_ref[...]

        def fill_rest(k, _):
            fill_pairs(wpr.at[k - 1], lambda dy, dx: wr_ref[k, dy, real_dx(dx)], CH)
            return 0

        lax.fori_loop(1, 5, fill_rest, 0)

        lane128 = lax.broadcasted_iota(jnp.int32, (CH, CH), 1)

        def fill_out(c, _):
            first = sx * c + (1 - sx) * (J + 1 - c) - 2
            tap = lax.rem(lane128, J) - first
            keep = (lane128 < 3 * J) & (tap >= 0) & (tap <= 2)
            placed = []
            for dy in range(3):
                placed.append(jnp.where(keep, pltpu.roll(wo_ref[dy], lax.rem(first + CH, CH), 1), 0.0))
            for i in range(RB + 2):
                total = jnp.zeros((CH, CH), f32)
                for dy in range(3):
                    ro = i - dy
                    if 0 <= ro < RB:
                        total = total + (pltpu.roll(placed[dy], 3 * J * ro, 1) if ro else placed[dy])
                k = pl.multiple_of((i * (J + 2) + c) * CH, CH)
                wpo[pl.ds(k, CH), :] = total.astype(bf)
            return 0

        lax.fori_loop(0, J + 2, fill_out, 0)

        act0[:, J + 1] = jnp.zeros((BC + 2, 2, SUB, CH), bf)
        act1[:, J + 1] = jnp.zeros((BC + 2, 2, SUB, CH), bf)
        act[:, J + 1] = jnp.zeros((R + 2, SUB, CH), bf)

        def scales(l, g):
            per = 8 if kind(l) == 0 else 4
            far_copy(l, g).wait()
            for half in range(halves(l)):
                x = st_sum[kind(l) % 2, g, half] + st_far[kind(l) % 2, g, half]
                k = 1
                while k < per:
                    x = x + jnp.where((lane8 & k) == 0, pltpu.roll(x, CH - k, 1), pltpu.roll(x, k, 1))
                    k *= 2
                flip = pltpu.roll(x, 4, 0)
                mean = jnp.where(sub8 < 4, x, flip) / (count * per)
                var = jnp.where(sub8 < 4, flip, x) / (count * per) - mean * mean
                if kind(l) == 0:
                    pair = n0_ref[:, half * CH:(half + 1) * CH].astype(f32)
                else:
                    pair = nr_ref[index(l) - 1].astype(f32)
                s = lax.rsqrt(var + GN_EPS) * pair[0:1]
                b = pair[1:2] - mean * s
                sb[0, half] = 0.5 * jnp.concatenate([s, s], axis=0)
                sb[1, half] = 0.5 * jnp.concatenate([b, b], axis=0)

        def finish_halo(l, g):
            x = xbuf(l)
            for c in halo_copies(l, g):
                c.wait()
            row, cor = halo_bufs(l, g)
            for side in range(2):
                shift = NS if side == 0 else SUB - NS
                outer = (sub16 < NS) if side == 0 else (sub16 >= SUB - NS)
                for j in range(J + 1):
                    for half in range(halves(l)):
                        own = x[g, R if side == 0 else 1, j, half].astype(f32)
                        far = (row[side, j - 1, half] if j else cor[side, half]).astype(f32)
                        v = jnp.where(outer, pltpu.roll(far, shift, 0), pltpu.roll(own, shift, 0))
                        x[g, 0 if side == 0 else R + 1, j, half] = v.astype(bf)

        def silu(x, half):
            u = x * sb[0, half] + sb[1, half]
            return u + u * jnp.tanh(u)

        top = (sub16 < NS) & (sy == 0)
        bottom = (sub16 >= SUB - NS) & (sy == 3)

        def activate(l, g, b, dst):
            x = xbuf(l)
            nb = R // BC
            for i in range(BC + 2):
                for half in range(halves(l)):
                    v = silu(x[g, b * BC + i, :, half].astype(f32), half)
                    if i == 0:
                        v = jnp.where(top & (b == 0), 0.0, v)
                    if i == BC + 1:
                        v = jnp.where(bottom & (b == nb - 1), 0.0, v)
                    dst[i, 0:J + 1, half] = v.astype(bf)

        def conv(l, g):
            wp = wp1 if kind(l) == 0 else (wp2 if kind(l) == 1 else wpr.at[index(l) - 2])
            out = xbuf(after(l))
            bias = bias_rows[pl.ds(index(l), 1), :]
            bias = jnp.broadcast_to(bias.reshape(1, 1, CH), (BC, SUB, CH))

            def block(b, src, one, two):
                r0 = b * BC
                rows = []
                for q in range(J // 2):
                    taps = []
                    for dy in range(3):
                        for d4 in range(4):
                            for half in range(halves(l)):
                                taps.append(src[dy:dy + BC, 2 * q + d4, half].reshape(BC * SUB, CH))
                    if kind(l) == 1:
                        for s in range(2):
                            for half in range(2):
                                taps.append(a_buf[g, pl.ds(r0 + 1, BC), 2 * q + s + 1, half].reshape(BC * SUB, CH))
                    rows.append(jnp.concatenate(taps, axis=1))
                lhs = jnp.concatenate(rows, axis=0)
                acc = jnp.dot(lhs, wp[...], preferred_element_type=f32)
                for q in range(J // 2):
                    for s in range(2):
                        at = (g, pl.ds(r0 + 1, BC), 2 * q + s + 1, 0)
                        v = acc[q * BC * SUB:(q + 1) * BC * SUB, s * CH:(s + 1) * CH].reshape(BC, SUB, CH) + bias
                        if kind(l) == 3:
                            v = v + out[at].astype(f32)
                        v = v.astype(bf)
                        out[at] = v
                        v = v.astype(f32)
                        one = one + jnp.sum(v, axis=0)
                        two = two + jnp.sum(v * v, axis=0)
                return one, two

            nb = R // BC
            activate(l, g, 0, act0)

            def step(i, carry):
                one, two = carry
                activate(l, g, 2 * i + 1, act1)
                one, two = block(2 * i, act0, one, two)
                activate(l, g, lax.rem(2 * i + 2, nb), act0)
                return block(2 * i + 1, act1, one, two)

            z = jnp.zeros((SUB, CH), f32)
            one, two = lax.fori_loop(0, nb // 2, step, (z, z))
            sacc[0, 0] = one
            sacc[1, 0] = two

        def head(g):
            x = h_buf
            nb = R // RB

            def row(r, _):
                for k in range(2):
                    act[2 * r + k, 0:J + 1] = silu(x[g, 2 * r + k, :, 0].astype(f32), 0).astype(bf)
                return 0

            lax.fori_loop(0, R // 2 + 1, row, 0)
            act[0, 0:J + 1] = jnp.where(top, 0.0, act[0, 0:J + 1].astype(f32)).astype(bf)
            act[R + 1, 0:J + 1] = jnp.where(bottom, 0.0, act[R + 1, 0:J + 1].astype(f32)).astype(bf)
            taps = []
            for i in range(RB + 2):
                for c in range(J + 2):
                    taps.append(jnp.concatenate([act[RB * b + i, c] for b in range(nb)], axis=0))
            acc = jnp.dot(jnp.concatenate(taps, axis=1), wpo[...], preferred_element_type=f32)
            acc = acc + bo_ref[...]
            for ro in range(RB):
                v = pltpu.roll(acc, CH - 3 * J * ro, 1) if ro else acc
                y_ref[g, :, ro] = v.reshape(nb, SUB, CH)

        biases = bias_ref[...].astype(f32)
        bias_rows[0:7] = biases
        bias_rows[1:2] = biases[1:2] + biases[6:7]

        def layer(l):
            def phase(g, _):
                if kind(l) > 0:
                    @pl.when(g == 1)
                    def _():
                        relay_sums(l, NG - 1)

                scales(l, g)
                finish_halo(l, g)
                if kind(l) == LAYERS - 1:
                    head(g)
                    return 0
                conv(l, g)
                push_sums(after(l), g)

                @pl.when(g > 0)
                def _():
                    relay_sums(after(l), g - 1)

                for c in halo_copies(after(l), g):
                    c.start()
                return 0

            lax.fori_loop(0, NG, phase, 0)

        layer(0)
        layer(1)

        def resnet(k, _):
            layer((2, 2 * k + 2))
            layer((3, 2 * k + 3))
            return 0

        lax.fori_loop(0, 2, resnet, 0)
        layer(6)

    def to_planes(x_ref, o_ref):
        rows = x_ref.shape[1] // SUB
        for i in range(NS):
            parts = [x_ref[0, pl.ds(p * NS + i, rows, stride=SUB), :] for p in range(NG)]
            flat = jnp.transpose(jnp.concatenate(parts, axis=0))
            o_ref[i] = flat[0:3 * J].reshape(3, J, NG * rows)

    def local_decode(act_in, norm_first, w_first, w_short, norm_rest, w_rest, bias_rest, w_out, bias_out):
        n, h, w, cin = act_in.shape
        rr = h // NG
        a = act_in.reshape(n, NG, rr, w, cin)
        f32 = jnp.float32
        lanes = jnp.arange(CH)[None, None, :]
        place = (lanes == (J * jnp.arange(3)[None, :, None] + 2 - jnp.arange(3)[:, None, None])).astype(jnp.bfloat16)
        wo = jnp.einsum("yxco,xol->ycl", w_out, place, preferred_element_type=f32)
        bo = jnp.tile(jnp.pad(jnp.repeat(bias_out.astype(f32), J), (0, 0)), RB)
        bo = jnp.pad(bo, (0, CH - 3 * J * RB)).reshape(1, CH)
        vm = pl.BlockSpec(memory_space=pltpu.VMEM)
        bf = jnp.bfloat16
        dma = pltpu.SemaphoreType.DMA
        y = pl.pallas_call(
            kernel,
            out_shape=jax.ShapeDtypeStruct((NG, rr // RB, RB, SUB, CH), f32),
            in_specs=[pl.BlockSpec(memory_space=pl.ANY)] + [vm] * 8,
            out_specs=vm,
            scratch_shapes=[
                pltpu.VMEM((NG, rr + 2, J + 1, 2, SUB, CH), bf),
                pltpu.VMEM((NG, rr + 2, J + 1, 1, SUB, CH), bf),
                pltpu.VMEM((NG, rr + 2, J + 1, 1, SUB, CH), bf),
                pltpu.VMEM((NG, 2, J, 2, SUB, CH), bf),
                pltpu.VMEM((2, NG, 2, J, 1, SUB, CH), bf),
                pltpu.VMEM((NG, 2, 2, SUB, CH), bf),
                pltpu.VMEM((2, NG, 2, 1, SUB, CH), bf),
                pltpu.VMEM((BC + 2, J + 2, 2, SUB, CH), bf),
                pltpu.VMEM((BC + 2, J + 2, 2, SUB, CH), bf),
                pltpu.VMEM((rr + 2, J + 2, SUB, CH), bf),
                pltpu.VMEM((TAPS * CIN, CIN), bf),
                pltpu.VMEM((2048, CIN), bf),
                pltpu.VMEM((NG, TAPS * CH, CIN), bf),
                pltpu.VMEM(((RB + 2) * (J + 2) * CH, CH), bf),
                pltpu.VMEM((2, NS, NG, RC, J, CIN), bf),
                pltpu.VMEM((2, 2, SUB * J, CH), f32),
                pltpu.VMEM((8, CH), f32),
                pltpu.VMEM((2, 2, SUB, CH), f32),
                pltpu.VMEM((2, NG, 2, 8, CH), f32),
                pltpu.VMEM((2, NG, 3, 2, 8, CH), f32),
                pltpu.VMEM((2, NG, 2, 8, CH), f32),
                pltpu.VMEM((2, NG, 2, 8, CH), f32),
                pltpu.VMEM((2, 2, SUB, CH), f32),
                dma((2,)),
                dma((LAYERS, NG)), dma((LAYERS, NG)),
                dma((LAYERS, NG, 2)), dma((LAYERS, NG, 2)),
                dma((LAYERS, NG, 2)), dma((LAYERS, NG, 2)),
                dma((LAYERS, NG, 3)), dma((LAYERS, NG, 3)),
                dma((LAYERS, NG)), dma((LAYERS, NG)),
            ],
            compiler_params=pltpu.CompilerParams(collective_id=0, has_side_effects=True, vmem_limit_bytes=67043328),
            name="decode",
        )(a, w_first, w_rest, w_short, wo, norm_first, norm_rest, bias_rest, bo)
        y = y.reshape(NG, rr * SUB, CH)
        y = pl.pallas_call(
            to_planes,
            grid=(NG,),
            out_shape=jax.ShapeDtypeStruct((n, 3, J, h), f32),
            in_specs=[pl.BlockSpec((1, rr * SUB, CH), lambda g: (g, 0, 0))],
            out_specs=pl.BlockSpec((NS, 3, J, h), lambda g: (g, 0, 0, 0)),
            name="to_planes",
        )(y)
        return jnp.transpose(y, (0, 3, 2, 1))

    return jax.shard_map(local_decode, mesh=mesh, in_specs=(tile_spec,) + (rep,) * 8, out_specs=tile_spec, check_vma=False)
```

time: 820 us -> 216 us (0.26)
  matrix products: 278 us -> 1.63 us
  Pallas kernels: 0 us -> 212 us
  waiting for transfers between devices: 207 us -> 0 us
  blocking collectives: 160 us -> 0 us
  other arithmetic: 108 us -> 0.08 us
  starting transfers between devices: 50.2 us -> 0 us
    conv_general_dilated x7 -> x0, matrix products: 257 us -> none  [conv_tile(): lax.conv_general_dilated(add_border(act_map), kernel, (1, 1), ((0, 0), (0...]
    pallas_call x0 -> x2, Pallas kernels: none -> 212 us  [the longest x1 208 us: local_decode(): pl.pallas_call(kernel, out_shape=jax.ShapeDtypeStruct((NG, rr // RB, RB,...]
    ppermute x28 -> x0, waiting for transfers between devices: 207 us -> none  [the longest x7 145 us: add_border(): left_col = lax.ppermute(tall[:, :, -1:], 'sx', to_right)]
    psum x7 -> x0, blocking collectives: 160 us -> none  [group_norm_act(): totals = lax.psum(jnp.stack([sum_one, sum_two], axis=-1), ('sy', 'sx'))]
    convert_element_type x10 -> x0, other arithmetic: 75.1 us -> none  [the longest x7 74.5 us: group_norm_act(): jax.nn.silu(act_map.astype(jnp.float32) * chan_scale[:, None, None, :] +...]
    ppermute x28 -> x0, starting transfers between devices: 50.2 us -> none  [the longest x7 22.3 us: add_border(): left_col = lax.ppermute(tall[:, :, -1:], 'sx', to_right)]
    reduce_sum x15 -> x0, other arithmetic: 30.2 us -> none  [the longest x8 29.9 us: group_norm_act(): jnp.sum(act_map, axis=(1, 2), dtype=jnp.float32)]
    dot_general x1, matrix products: 21.3 us -> 1.63 us  [local_decode(): wo = jnp.einsum('yxco,xol->ycl', w_out, place, preferred_element_type=f32)]
  transfers between devices with their start and end apart: 28 -> 0, of which waited for: 20 -> 0; matrix products, arithmetic and copies ran while one was open for 3% -> 0% of each run, Pallas kernels for 0% -> 0%
where the time goes in v2:
time: 216 us; the launch traced here: 215 us
  Pallas kernels  212 us (98%)
    pallas_call x1, Pallas kernels, local_decode(): pl.pallas_call(kernel, out_shape=jax.ShapeDtypeStruct((NG, rr // RB, RB,...  208 us

profile of v2, /device:TPU:0, one launch (start us, length us, event | category | flops | bytes accessed | tf_op | source)
XLA Modules:
  0.0 215.1 jit_solution(11428425621433979126)
XLA Ops:
  0.0 0.1 iota_subtract_fusion
  0.1 0.7 broadcast_in_dim.2
  0.8 0.1 tile.11
  0.9 0.1 tile.13
  1.0 0.5 pad_bitcast_fusion.bo_ref
  1.5 1.6 convolution_bitcast_fusion.wo_ref
  3.1 208.1 %decode.1 = f32[4,16,4,16,128]{4,3,2,1,0:T(8,128)} custom-call(bf16[16,4,64,8,256]{4,3,2,1,0:T(8,128)(2,1)} %bitcast.12, bf16[3,3,256,128]{3,2,1,0:T(8,128)(2,1)} %w1_ref.1, bf16[5,3,3,128,128]{4,3,2,1,0:T(8,128)(2,1)} %wr_ref.1, bf16[256,128]{1,0:T(8,128)(2,1)} %ws_ref.1, f32[3,128,128]{2,1,0:T(8,128)} %convolution_bitcast_fusion.wo_ref, ...), custom_call_target="tpu_custom_call" | custom-call | tf_op jit(solution)/shard_map/decode/pallas_call | solution.py:414
  211.3 3.8 %to_planes.1 = f32[16,3,8,256]{3,2,1,0:T(8,128)} custom-call(f32[4,1024,128]{2,1,0:T(8,128)} %bitcast.13), custom_call_target="tpu_custom_call" | custom-call | tf_op jit(solution)/shard_map/to_planes/pallas_call | solution.py:454
  (2 shorter events, 0.0 us)

commit v3 on v2

--- a/solution.py
+++ b/solution.py
@@ -11,23 +11,24 @@
 NS = 4
 SUB = 16
 J = 8
-BC = 8
+BC = 16
 RC = 8
 RB = 4
+HR = 6
 LAYERS = 7
 CH = 128
 CIN = 256
-TAPS = 12
+TAPS = 14
 
 
 def solution(mesh):
     tile_spec = P("dp", "sy", "sx", None)
     rep = P()
 
-    def kernel(a_hbm, w1_ref, wr_ref, ws_ref, wo_ref, n0_ref, nr_ref, bias_ref, bo_ref, y_ref,
-               a_buf, t_buf, h_buf, rowa, rowx, cora, corx, act0, act1, act, wp1, wp2, wpr, wpo,
-               raw, tmp, bias_rows, sacc, st_own, st_in, st_sum, st_far, sb,
-               raw_sem, col_s, col_r, row_s, row_r, cor_s, cor_r, st_s, st_r, far_s, far_r):
+    def kernel(a_hbm, w1_ref, wr_ref, ws_ref, wo_ref, n0_ref, nr_ref, bias_ref, y_ref,
+               a_buf, t_buf, h_buf, rowa, rowx, cora, corx, act0, act1, wp1, wp2, wpr, wpo,
+               raw, tmp, ps_out, ps_in, bias_rows, sacc, st_own, st_in, st_sum, st_far, sb,
+               raw_sem, col_s, col_r, row_s, row_r, cor_s, cor_r, st_s, st_r, far_s, far_r, ps_s, ps_r, pc_s, pc_r):
         sx = lax.axis_index("sx")
         sy = lax.axis_index("sy")
         px = 1 - sx
@@ -73,16 +74,47 @@
                 return rowa.at[g], cora.at[g]
             return rowx.at[kind(l) % 2, g], corx.at[kind(l) % 2, g]
 
-        def halo_copies(l, g):
+        def row_copies(l, g):
             x = xbuf(l)
-            row, cor = halo_bufs(l, g)
+            row, _ = halo_bufs(l, g)
             return [
                 rcopy(x.at[g, R, pl.ds(1, J)], row.at[0], row_s.at[index(l), g, 0], row_r.at[index(l), g, 0], {"sx": sx, "sy": dn}),
                 rcopy(x.at[g, 1, pl.ds(1, J)], row.at[1], row_s.at[index(l), g, 1], row_r.at[index(l), g, 1], {"sx": sx, "sy": up}),
+            ]
+
+        def piece_copy(ch):
+            rows = pl.ds(ch * RC + 1, RC)
+            return rcopy(a_buf.at[0, rows, 1], a_buf.at[0, rows, 0], pc_s.at[ch], pc_r.at[ch], {"sx": px, "sy": sy})
+
+        def col_copy(l, g):
+            x = xbuf(l)
+            return rcopy(x.at[g, pl.ds(1, R), 1], x.at[g, pl.ds(1, R), 0], col_s.at[index(l), g], col_r.at[index(l), g], {"sx": px, "sy": sy})
+
+        def corner_copies(l, g):
+            x = xbuf(l)
+            _, cor = halo_bufs(l, g)
+            return [
                 rcopy(x.at[g, R, 1], cor.at[0], cor_s.at[index(l), g, 0], cor_r.at[index(l), g, 0], {"sx": px, "sy": dn}),
                 rcopy(x.at[g, 1, 1], cor.at[1], cor_s.at[index(l), g, 1], cor_r.at[index(l), g, 1], {"sx": px, "sy": up}),
-                rcopy(x.at[g, pl.ds(1, R), 1], x.at[g, pl.ds(1, R), 0], col_s.at[index(l), g], col_r.at[index(l), g], {"sx": px, "sy": sy}),
             ]
+
+        def start_halo(l, g):
+            for c in row_copies(l, g):
+                c.start()
+            if kind(l) == 2:
+                @pl.when(index(l) < LAYERS - 1)
+                def _():
+                    for c in corner_copies(l, g) + [col_copy(l, g)]:
+                        c.start()
+            else:
+                for c in corner_copies(l, g):
+                    c.start()
+                if kind(l) == 0:
+                    @pl.when(g > 0)
+                    def _():
+                        col_copy(l, g).start()
+                else:
+                    col_copy(l, g).start()
 
         def near_copies(l, g):
             nh = halves(l)
@@ -153,13 +185,18 @@
                 for half in range(2):
                     sacc[0, half] = sacc[0, half] + ones[half]
                     sacc[1, half] = sacc[1, half] + twos[half]
+
+                @pl.when(g == 0)
+                def _():
+                    @pl.when(ch == 0)
+                    def _():
+                        pl.semaphore_wait(barrier, len(friends))
+
+                    piece_copy(ch).start()
+
                 return 0
 
             lax.fori_loop(0, nchunk, load_chunk, 0)
-
-            @pl.when(g == 0)
-            def _():
-                pl.semaphore_wait(barrier, len(friends))
 
             push_sums(0, g)
 
@@ -167,62 +204,71 @@
             def _():
                 relay_sums(0, g - 1)
 
-            for c in halo_copies(0, g):
-                c.start()
+            start_halo(0, g)
             return 0
 
         lax.fori_loop(0, NG, load_group, 0)
 
-        def fill_pairs(dst, get, ch):
+        def fill_block(dst, w, ch, extra):
             zero = jnp.zeros((ch, CH), bf)
+
+            def tap(dy, dx):
+                return w[dy, sx * dx + (1 - sx) * (2 - dx)]
+
+            parts = [(tap(0, 0), zero), (zero, tap(0, 2))]
             for dy in range(3):
-                for d4 in range(4):
-                    k = (dy * 4 + d4) * ch
-                    dst[k:k + ch, 0:CH] = get(dy, d4) if d4 < 3 else zero
-                    dst[k:k + ch, CH:CIN] = get(dy, d4 - 1) if d4 > 0 else zero
-
-        def real_dx(dx):
-            return sx * dx + (1 - sx) * (2 - dx)
-
-        fill_pairs(wp1, lambda dy, dx: w1_ref[dy, real_dx(dx)], CIN)
+                parts += [(tap(dy, 1), tap(dy, 0)), (tap(dy, 2), tap(dy, 1))]
+            tail = [(tap(2, 0), zero), (zero, tap(2, 2))]
+            for dx in (0, 2):
+                tail += [(tap(1, dx), tap(0, dx)), (tap(2, dx), tap(1, dx))]
+            k = 0
+            for group in (parts, extra, tail):
+                for left, right in group:
+                    size = left.shape[0]
+                    dst[k:k + size, 0:CH] = left
+                    dst[k:k + size, CH:CIN] = right
+                    k += size
+
+        fill_block(wp1, w1_ref, CIN, [])
         relay_sums(0, NG - 1)
-        fill_pairs(wp2, lambda dy, dx: wr_ref[0, dy, real_dx(dx)], CH)
-        zs = jnp.zeros((CIN, CH), bf)
-        wp2[1536:1792, 0:CH] = ws_ref[...]
-        wp2[1536:1792, CH:CIN] = zs
-        wp2[1792:2048, 0:CH] = zs
-        wp2[1792:2048, CH:CIN] = ws_ref[...]
+        fill_block(wp2, wr_ref.at[0], CH, [(ws_ref[...], jnp.zeros((CIN, CH), bf)), (jnp.zeros((CIN, CH), bf), ws_ref[...])])
 
         def fill_rest(k, _):
-            fill_pairs(wpr.at[k - 1], lambda dy, dx: wr_ref[k, dy, real_dx(dx)], CH)
+            fill_block(wpr.at[k - 1], wr_ref.at[k], CH, [])
             return 0
 
         lax.fori_loop(1, 5, fill_rest, 0)
 
         lane128 = lax.broadcasted_iota(jnp.int32, (CH, CH), 1)
 
-        def fill_out(c, _):
-            first = sx * c + (1 - sx) * (J + 1 - c) - 2
-            tap = lax.rem(lane128, J) - first
-            keep = (lane128 < 3 * J) & (tap >= 0) & (tap <= 2)
-            placed = []
-            for dy in range(3):
-                placed.append(jnp.where(keep, pltpu.roll(wo_ref[dy], lax.rem(first + CH, CH), 1), 0.0))
+        def place_rows(c, placed, col):
             for i in range(RB + 2):
                 total = jnp.zeros((CH, CH), f32)
                 for dy in range(3):
                     ro = i - dy
                     if 0 <= ro < RB:
                         total = total + (pltpu.roll(placed[dy], 3 * J * ro, 1) if ro else placed[dy])
-                k = pl.multiple_of((i * (J + 2) + c) * CH, CH)
-                wpo[pl.ds(k, CH), :] = total.astype(bf)
+                k = pl.multiple_of((i * J + c) * CH, CH)
+                wpo[pl.ds(k, CH), col:col + CH] = total.astype(bf)
+
+        def fill_out(c, _):
+            first = sx * (c + 1) + (1 - sx) * (J - c) - 2
+            tap = lax.rem(lane128, J) - first
+            keep = (lane128 < 3 * J) & (tap >= 0) & (tap <= 2)
+            place_rows(c, [jnp.where(keep, pltpu.roll(wo_ref[dy], lax.rem(first + CH, CH), 1), 0.0) for dy in range(3)], 0)
+            for i in range(RB + 2):
+                k = pl.multiple_of((i * J + c) * CH, CH)
+                wpo[pl.ds(k, CH), CH:CIN] = jnp.zeros((CH, CH), bf)
             return 0
 
-        lax.fori_loop(0, J + 2, fill_out, 0)
-
-        act0[:, J + 1] = jnp.zeros((BC + 2, 2, SUB, CH), bf)
-        act1[:, J + 1] = jnp.zeros((BC + 2, 2, SUB, CH), bf)
-        act[:, J + 1] = jnp.zeros((R + 2, SUB, CH), bf)
+        lax.fori_loop(0, J, fill_out, 0)
+        edge = (J - 1) * (1 - sx)
+        far_edge = (J - 1) * sx
+        keep = (lane128 < 3 * J) & (lax.rem(lane128, J) == far_edge)
+        place_rows(0, [jnp.where(keep, pltpu.roll(wo_ref[dy], lax.rem(far_edge - 2 * (1 - sx) + CH, CH), 1), 0.0) for dy in range(3)], CH)
+
+        for block_map in (act0, act1):
+            block_map[:, :, J + 1] = jnp.zeros((BC // 2 + 1, 2, 2, SUB, CH), bf)
 
         def scales(l, g):
             per = 8 if kind(l) == 0 else 4
@@ -247,13 +293,28 @@
 
         def finish_halo(l, g):
             x = xbuf(l)
-            for c in halo_copies(l, g):
+            last = kind(l) == LAYERS - 1
+            for c in row_copies(l, g):
                 c.wait()
+            if not last:
+                for c in corner_copies(l, g):
+                    c.wait()
+            if kind(l) == 0:
+                @pl.when(g == 0)
+                def _():
+                    for ch in range(nchunk):
+                        piece_copy(ch).wait()
+
+                @pl.when(g > 0)
+                def _():
+                    col_copy(l, g).wait()
+            elif not last:
+                col_copy(l, g).wait()
             row, cor = halo_bufs(l, g)
             for side in range(2):
                 shift = NS if side == 0 else SUB - NS
                 outer = (sub16 < NS) if side == 0 else (sub16 >= SUB - NS)
-                for j in range(J + 1):
+                for j in range(1 if last else 0, J + 1):
                     for half in range(halves(l)):
                         own = x[g, R if side == 0 else 1, j, half].astype(f32)
                         far = (row[side, j - 1, half] if j else cor[side, half]).astype(f32)
@@ -277,7 +338,7 @@
                         v = jnp.where(top & (b == 0), 0.0, v)
                     if i == BC + 1:
                         v = jnp.where(bottom & (b == nb - 1), 0.0, v)
-                    dst[i, 0:J + 1, half] = v.astype(bf)
+                    dst[i // 2, i % 2, 0:J + 1, half] = v.astype(bf)
 
         def conv(l, g):
             wp = wp1 if kind(l) == 0 else (wp2 if kind(l) == 1 else wpr.at[index(l) - 2])
@@ -285,26 +346,48 @@
             bias = bias_rows[pl.ds(index(l), 1), :]
             bias = jnp.broadcast_to(bias.reshape(1, 1, CH), (BC, SUB, CH))
 
+            half_rows = BC // 2
+            ch = CH * halves(l)
+            mid = 6 * ch + (2 * CIN if kind(l) == 1 else 0)
+
             def block(b, src, one, two):
                 r0 = b * BC
-                rows = []
-                for q in range(J // 2):
-                    taps = []
+                m = half_rows * SUB
+
+                def pixel(t, col):
+                    return [src[t // 2:t // 2 + half_rows, t % 2, col, half].reshape(m, CH) for half in range(halves(l))]
+
+                def stack(columns):
+                    return jnp.concatenate([jnp.concatenate(columns(2 * q), axis=1) for q in range(J // 2)], axis=0)
+
+                skips = []
+                if kind(l) == 1:
+                    for c in range(J):
+                        skips.append([a_buf[g, pl.ds(r0 + 1, BC), c + 1, half].reshape(half_rows, 2, SUB, CH) for half in range(2)])
+
+                def taps(r, q2):
+                    own = []
                     for dy in range(3):
-                        for d4 in range(4):
-                            for half in range(halves(l)):
-                                taps.append(src[dy:dy + BC, 2 * q + d4, half].reshape(BC * SUB, CH))
+                        own += pixel(r + dy, q2 + 1) + pixel(r + dy, q2 + 2)
                     if kind(l) == 1:
-                        for s in range(2):
-                            for half in range(2):
-                                taps.append(a_buf[g, pl.ds(r0 + 1, BC), 2 * q + s + 1, half].reshape(BC * SUB, CH))
-                    rows.append(jnp.concatenate(taps, axis=1))
-                lhs = jnp.concatenate(rows, axis=0)
-                acc = jnp.dot(lhs, wp[...], preferred_element_type=f32)
+                        own += [v[:, r:r + 1].reshape(m, CH) for c in range(2) for v in skips[q2 + c]]
+                    corner = pixel(3 * r, q2) + pixel(3 * r, q2 + 3)
+                    return own + corner if r else corner + own
+
+                def mm(lhs, start, size):
+                    return jnp.dot(lhs, wp[start:start + size, :], preferred_element_type=f32)
+
+                rows = [mm(stack(lambda q2: taps(r, q2)), 2 * ch * r, mid + 2 * ch) for r in range(2)]
+                base = mid + 4 * ch
+                sides = [mm(stack(lambda q2: pixel(1, q2 + 3 * s) + pixel(2, q2 + 3 * s)), base + 2 * ch * s, 2 * ch) for s in range(2)]
                 for q in range(J // 2):
                     for s in range(2):
+                        pair = []
+                        for r in range(2):
+                            v = rows[r][q * m:(q + 1) * m, s * CH:(s + 1) * CH] + sides[s][q * m:(q + 1) * m, r * CH:(r + 1) * CH]
+                            pair.append(v.reshape(half_rows, 1, SUB, CH))
+                        v = jnp.concatenate(pair, axis=1).reshape(BC, SUB, CH) + bias
                         at = (g, pl.ds(r0 + 1, BC), 2 * q + s + 1, 0)
-                        v = acc[q * BC * SUB:(q + 1) * BC * SUB, s * CH:(s + 1) * CH].reshape(BC, SUB, CH) + bias
                         if kind(l) == 3:
                             v = v + out[at].astype(f32)
                         v = v.astype(bf)
@@ -329,27 +412,45 @@
             sacc[0, 0] = one
             sacc[1, 0] = two
 
+        nblk = R // RB
+
+        def edge_copy(g):
+            return rcopy(ps_out.at[g], ps_in.at[g], ps_s.at[g], ps_r.at[g], {"sx": px, "sy": sy})
+
+        def head_act(g):
+            def rows(step, _):
+                for k in range(HR):
+                    r = HR * step + k
+                    t_buf[g, r, 0:J, 0] = silu(h_buf[g, r, 1:J + 1, 0].astype(f32), 0).astype(bf)
+                return 0
+
+            lax.fori_loop(0, (R + 2) // HR, rows, 0)
+            for r, border in ((0, top), (R + 1, bottom)):
+                t_buf[g, r, 0:J, 0] = jnp.where(border, 0.0, t_buf[g, r, 0:J, 0].astype(f32)).astype(bf)
+
         def head(g):
-            x = h_buf
-            nb = R // RB
-
-            def row(r, _):
-                for k in range(2):
-                    act[2 * r + k, 0:J + 1] = silu(x[g, 2 * r + k, :, 0].astype(f32), 0).astype(bf)
-                return 0
-
-            lax.fori_loop(0, R // 2 + 1, row, 0)
-            act[0, 0:J + 1] = jnp.where(top, 0.0, act[0, 0:J + 1].astype(f32)).astype(bf)
-            act[R + 1, 0:J + 1] = jnp.where(bottom, 0.0, act[R + 1, 0:J + 1].astype(f32)).astype(bf)
             taps = []
             for i in range(RB + 2):
-                for c in range(J + 2):
-                    taps.append(jnp.concatenate([act[RB * b + i, c] for b in range(nb)], axis=0))
+                for c in range(J):
+                    taps.append(jnp.concatenate([t_buf[g, RB * b + i, c, 0] for b in range(nblk)], axis=0))
             acc = jnp.dot(jnp.concatenate(taps, axis=1), wpo[...], preferred_element_type=f32)
-            acc = acc + bo_ref[...]
-            for ro in range(RB):
-                v = pltpu.roll(acc, CH - 3 * J * ro, 1) if ro else acc
-                y_ref[g, :, ro] = v.reshape(nb, SUB, CH)
+            y_ref[g] = acc[:, 0:CH].reshape(nblk, SUB, CH)
+            for part in range(nblk // J):
+                total = jnp.zeros((SUB, CH), f32)
+                for k in range(J):
+                    b = part * J + k
+                    total = total + pltpu.roll(acc[b * SUB:(b + 1) * SUB, CH:CIN], lax.rem(k - far_edge + CH, CH), 1)
+                ps_out[g, part] = total
+            edge_copy(g).start()
+
+        def add_edges(g, _):
+            edge_copy(g).wait()
+            lane16 = lax.broadcasted_iota(jnp.int32, (SUB, CH), 1)
+            mine = (lane16 < 3 * J * RB) & (lax.rem(lane16, J) == edge)
+            for b in range(nblk):
+                v = pltpu.roll(ps_in[g, b // J], lax.rem(edge - b % J + CH, CH), 1)
+                y_ref[g, b] = y_ref[g, b] + jnp.where(mine, v, 0.0)
+            return 0
 
         biases = bias_ref[...].astype(f32)
         bias_rows[0:7] = biases
@@ -364,9 +465,6 @@
 
                 scales(l, g)
                 finish_halo(l, g)
-                if kind(l) == LAYERS - 1:
-                    head(g)
-                    return 0
                 conv(l, g)
                 push_sums(after(l), g)
 
@@ -374,8 +472,7 @@
                 def _():
                     relay_sums(after(l), g - 1)
 
-                for c in halo_copies(after(l), g):
-                    c.start()
+                start_halo(after(l), g)
                 return 0
 
             lax.fori_loop(0, NG, phase, 0)
@@ -389,14 +486,34 @@
             return 0
 
         lax.fori_loop(0, 2, resnet, 0)
-        layer(6)
-
-    def to_planes(x_ref, o_ref):
-        rows = x_ref.shape[1] // SUB
+        def last(g, _):
+            @pl.when(g == 1)
+            def _():
+                relay_sums(LAYERS - 1, NG - 1)
+
+            scales(LAYERS - 1, g)
+            finish_halo(LAYERS - 1, g)
+            head_act(g)
+            head(g)
+            return 0
+
+        lax.fori_loop(0, NG, last, 0)
+        lax.fori_loop(0, NG, add_edges, 0)
+
+    def to_planes(x_ref, b_ref, o_ref, ys):
+        bias = b_ref[...].astype(jnp.float32)
+        blocks = x_ref.shape[1]
+        rows = blocks * RB
+        v = x_ref[0].reshape(blocks * SUB, CH)
+        for ro in range(RB):
+            u = pltpu.roll(v, CH - 3 * J * ro, 1) if ro else v
+            for b in range(blocks):
+                ys[(RB * b + ro) * SUB:(RB * b + ro + 1) * SUB] = u[b * SUB:(b + 1) * SUB]
         for i in range(NS):
-            parts = [x_ref[0, pl.ds(p * NS + i, rows, stride=SUB), :] for p in range(NG)]
+            parts = [ys[pl.ds(p * NS + i, rows, stride=SUB), :] for p in range(NG)]
             flat = jnp.transpose(jnp.concatenate(parts, axis=0))
-            o_ref[i] = flat[0:3 * J].reshape(3, J, NG * rows)
+            for c in range(3):
+                o_ref[i, c] = flat[c * J:(c + 1) * J] + bias[:, c:c + 1]
 
     def local_decode(act_in, norm_first, w_first, w_short, norm_rest, w_rest, bias_rest, w_out, bias_out):
         n, h, w, cin = act_in.shape
@@ -406,15 +523,15 @@
         lanes = jnp.arange(CH)[None, None, :]
         place = (lanes == (J * jnp.arange(3)[None, :, None] + 2 - jnp.arange(3)[:, None, None])).astype(jnp.bfloat16)
         wo = jnp.einsum("yxco,xol->ycl", w_out, place, preferred_element_type=f32)
-        bo = jnp.tile(jnp.pad(jnp.repeat(bias_out.astype(f32), J), (0, 0)), RB)
-        bo = jnp.pad(bo, (0, CH - 3 * J * RB)).reshape(1, CH)
         vm = pl.BlockSpec(memory_space=pltpu.VMEM)
         bf = jnp.bfloat16
         dma = pltpu.SemaphoreType.DMA
+        block_map = pltpu.VMEM((BC // 2 + 1, 2, J + 2, 2, SUB, CH), bf)
+        sides = dma((LAYERS, NG, 2))
         y = pl.pallas_call(
             kernel,
-            out_shape=jax.ShapeDtypeStruct((NG, rr // RB, RB, SUB, CH), f32),
-            in_specs=[pl.BlockSpec(memory_space=pl.ANY)] + [vm] * 8,
+            out_shape=jax.ShapeDtypeStruct((NG, rr // RB, SUB, CH), f32),
+            in_specs=[pl.BlockSpec(memory_space=pl.ANY)] + [vm] * 7,
             out_specs=vm,
             scratch_shapes=[
                 pltpu.VMEM((NG, rr + 2, J + 1, 2, SUB, CH), bf),
@@ -424,15 +541,15 @@
                 pltpu.VMEM((2, NG, 2, J, 1, SUB, CH), bf),
                 pltpu.VMEM((NG, 2, 2, SUB, CH), bf),
                 pltpu.VMEM((2, NG, 2, 1, SUB, CH), bf),
-                pltpu.VMEM((BC + 2, J + 2, 2, SUB, CH), bf),
-                pltpu.VMEM((BC + 2, J + 2, 2, SUB, CH), bf),
-                pltpu.VMEM((rr + 2, J + 2, SUB, CH), bf),
+                block_map, block_map,
                 pltpu.VMEM((TAPS * CIN, CIN), bf),
-                pltpu.VMEM((2048, CIN), bf),
+                pltpu.VMEM((TAPS * CH + 2 * CIN, CIN), bf),
                 pltpu.VMEM((NG, TAPS * CH, CIN), bf),
-                pltpu.VMEM(((RB + 2) * (J + 2) * CH, CH), bf),
+                pltpu.VMEM(((RB + 2) * J * CH, CIN), bf),
                 pltpu.VMEM((2, NS, NG, RC, J, CIN), bf),
                 pltpu.VMEM((2, 2, SUB * J, CH), f32),
+                pltpu.VMEM((NG, rr // RB // J, SUB, CH), f32),
+                pltpu.VMEM((NG, rr // RB // J, SUB, CH), f32),
                 pltpu.VMEM((8, CH), f32),
                 pltpu.VMEM((2, 2, SUB, CH), f32),
                 pltpu.VMEM((2, NG, 2, 8, CH), f32),
@@ -442,23 +559,24 @@
                 pltpu.VMEM((2, 2, SUB, CH), f32),
                 dma((2,)),
                 dma((LAYERS, NG)), dma((LAYERS, NG)),
-                dma((LAYERS, NG, 2)), dma((LAYERS, NG, 2)),
-                dma((LAYERS, NG, 2)), dma((LAYERS, NG, 2)),
+                sides, sides, sides, sides,
                 dma((LAYERS, NG, 3)), dma((LAYERS, NG, 3)),
                 dma((LAYERS, NG)), dma((LAYERS, NG)),
+                dma((NG,)), dma((NG,)),
+                dma((rr // RC,)), dma((rr // RC,)),
             ],
             compiler_params=pltpu.CompilerParams(collective_id=0, has_side_effects=True, vmem_limit_bytes=67043328),
             name="decode",
-        )(a, w_first, w_rest, w_short, wo, norm_first, norm_rest, bias_rest, bo)
-        y = y.reshape(NG, rr * SUB, CH)
+        )(a, w_first, w_rest, w_short, wo, norm_first, norm_rest, bias_rest)
         y = pl.pallas_call(
             to_planes,
             grid=(NG,),
             out_shape=jax.ShapeDtypeStruct((n, 3, J, h), f32),
-            in_specs=[pl.BlockSpec((1, rr * SUB, CH), lambda g: (g, 0, 0))],
+            in_specs=[pl.BlockSpec((1, rr // RB, SUB, CH), lambda g: (g, 0, 0, 0)), pl.BlockSpec((1, 3), lambda g: (0, 0))],
             out_specs=pl.BlockSpec((NS, 3, J, h), lambda g: (g, 0, 0, 0)),
+            scratch_shapes=[pltpu.VMEM((rr * SUB, CH), f32)],
             name="to_planes",
-        )(y)
+        )(y, bias_out.reshape(1, 3))
         return jnp.transpose(y, (0, 3, 2, 1))
 
     return jax.shard_map(local_decode, mesh=mesh, in_specs=(tile_spec,) + (rep,) * 8, out_specs=tile_spec, check_vma=False)

time: 216 us -> 202 us (0.935)
  Pallas kernels: 212 us -> 199 us
    pallas_call x1, Pallas kernels: 208 us -> 196 us  [local_decode(): pl.pallas_call(kernel, out_shape=jax.ShapeDtypeStruct((NG, rr // RB, SUB,...]
where the time goes in v3:
time: 202 us; the launch traced here: 201 us
  Pallas kernels  199 us (99%)
    pallas_call x1, Pallas kernels, local_decode(): pl.pallas_call(kernel, out_shape=jax.ShapeDtypeStruct((NG, rr // RB, SUB,...  196 us

profile of v3, /device:TPU:0, one launch (start us, length us, event | category | flops | bytes accessed | tf_op | source)
XLA Modules:
  0.0 201.2 jit_solution(13050848763892919753)
XLA Ops:
  0.0 0.1 iota_subtract_fusion
  0.1 1.6 convolution_bitcast_fusion.wo_ref
  1.7 195.6 %decode.1.x_ref = f32[4,16,16,128]{3,2,1,0:T(8,128)} custom-call(bf16[16,4,64,8,256]{4,3,2,1,0:T(8,128)(2,1)} %bitcast.10, bf16[3,3,256,128]{3,2,1,0:T(8,128)(2,1)} %w1_ref.1, bf16[5,3,3,128,128]{4,3,2,1,0:T(8,128)(2,1)} %wr_ref.1, bf16[256,128]{1,0:T(8,128)(2,1)} %ws_ref.1, f32[3,128,128]{2,1,0:T(8,128)} %convolution_bitcast_fusion.wo_ref, ...), custom_call_target="tpu_custom_call" | custom-call | tf_op jit(solution)/shard_map/decode/pallas_call | solution.py:531
  197.3 3.9 %to_planes.1 = f32[16,3,8,256]{3,2,1,0:T(8,128)} custom-call(f32[4,16,16,128]{3,2,1,0:T(8,128)} %decode.1.x_ref, bf16[1,3]{1,0:T(2,128)(2,1)} %bitcast.11), custom_call_target="tpu_custom_call" | custom-call | tf_op jit(solution)/shard_map/to_planes/pallas_call | solution.py:571
  (1 shorter events, 0.0 us)

commit v4 on v3

--- a/solution.py
+++ b/solution.py
@@ -13,6 +13,7 @@
 J = 8
 BC = 16
 RC = 8
+SLOTS = 4
 RB = 4
 HR = 6
 LAYERS = 7
@@ -49,7 +50,8 @@
                 a_hbm.at[pl.ds(g * NS, NS), :, pl.ds(chunk * RC, RC)], raw.at[slot], raw_sem.at[slot])
 
         nchunk = R // RC
-        raw_copy(0, 0, 0).start()
+        for ahead in range(SLOTS - 1):
+            raw_copy(0, ahead, ahead).start()
 
         def rcopy(src, dst, ss, rs, dev):
             return pltpu.make_async_remote_copy(src_ref=src, dst_ref=dst, send_sem=ss, recv_sem=rs, device_id=dev, device_id_type=MESH)
@@ -158,12 +160,12 @@
 
             def load_chunk(ch, _):
                 step = g * nchunk + ch
-                slot = lax.rem(step, 2)
-                nxt = step + 1
+                slot = lax.rem(step, SLOTS)
+                nxt = step + SLOTS - 1
 
                 @pl.when(nxt < NG * nchunk)
                 def _():
-                    raw_copy(lax.div(nxt, nchunk), lax.rem(nxt, nchunk), lax.rem(nxt, 2)).start()
+                    raw_copy(lax.div(nxt, nchunk), lax.rem(nxt, nchunk), lax.rem(nxt, SLOTS)).start()
 
                 raw_copy(g, ch, slot).wait()
                 ones = [jnp.zeros((SUB, CH), f32) for _ in range(2)]
@@ -402,10 +404,11 @@
 
             def step(i, carry):
                 one, two = carry
+                one, two = block(2 * i, act0, one, two)
                 activate(l, g, 2 * i + 1, act1)
-                one, two = block(2 * i, act0, one, two)
+                one, two = block(2 * i + 1, act1, one, two)
                 activate(l, g, lax.rem(2 * i + 2, nb), act0)
-                return block(2 * i + 1, act1, one, two)
+                return one, two
 
             z = jnp.zeros((SUB, CH), f32)
             one, two = lax.fori_loop(0, nb // 2, step, (z, z))
@@ -546,7 +549,7 @@
                 pltpu.VMEM((TAPS * CH + 2 * CIN, CIN), bf),
                 pltpu.VMEM((NG, TAPS * CH, CIN), bf),
                 pltpu.VMEM(((RB + 2) * J * CH, CIN), bf),
-                pltpu.VMEM((2, NS, NG, RC, J, CIN), bf),
+                pltpu.VMEM((SLOTS, NS, NG, RC, J, CIN), bf),
                 pltpu.VMEM((2, 2, SUB * J, CH), f32),
                 pltpu.VMEM((NG, rr // RB // J, SUB, CH), f32),
                 pltpu.VMEM((NG, rr // RB // J, SUB, CH), f32),
@@ -557,7 +560,7 @@
                 pltpu.VMEM((2, NG, 2, 8, CH), f32),
                 pltpu.VMEM((2, NG, 2, 8, CH), f32),
                 pltpu.VMEM((2, 2, SUB, CH), f32),
-                dma((2,)),
+                dma((SLOTS,)),
                 dma((LAYERS, NG)), dma((LAYERS, NG)),
                 sides, sides, sides, sides,
                 dma((LAYERS, NG, 3)), dma((LAYERS, NG, 3)),

time: 202 us -> 202 us (level)
  no operation moved by 1% of the time
where the time goes in v4:
time: 202 us; the launch traced here: 201 us
  Pallas kernels  199 us (99%)
    pallas_call x1, Pallas kernels, local_decode(): pl.pallas_call(kernel, out_shape=jax.ShapeDtypeStruct((NG, rr // RB, SUB,...  196 us

profile of v4, /device:TPU:0, one launch (start us, length us, event | category | flops | bytes accessed | tf_op | source)
XLA Modules:
  0.0 201.2 jit_solution(10481042263163285151)
XLA Ops:
  0.0 0.1 iota_subtract_fusion
  0.1 1.6 convolution_bitcast_fusion.wo_ref
  1.7 195.6 %decode.1.x_ref = f32[4,16,16,128]{3,2,1,0:T(8,128)} custom-call(bf16[16,4,64,8,256]{4,3,2,1,0:T(8,128)(2,1)} %bitcast.10, bf16[3,3,256,128]{3,2,1,0:T(8,128)(2,1)} %w1_ref.1, bf16[5,3,3,128,128]{4,3,2,1,0:T(8,128)(2,1)} %wr_ref.1, bf16[256,128]{1,0:T(8,128)(2,1)} %ws_ref.1, f32[3,128,128]{2,1,0:T(8,128)} %convolution_bitcast_fusion.wo_ref, ...), custom_call_target="tpu_custom_call" | custom-call | tf_op jit(solution)/shard_map/decode/pallas_call | solution.py:534
  197.3 3.9 %to_planes.1 = f32[16,3,8,256]{3,2,1,0:T(8,128)} custom-call(f32[4,16,16,128]{3,2,1,0:T(8,128)} %decode.1.x_ref, bf16[1,3]{1,0:T(2,128)(2,1)} %bitcast.11), custom_call_target="tpu_custom_call" | custom-call | tf_op jit(solution)/shard_map/to_planes/pallas_call | solution.py:574
  (1 shorter events, 0.0 us)

commit v5 on v4

--- a/solution.py
+++ b/solution.py
@@ -469,13 +469,13 @@
                 scales(l, g)
                 finish_halo(l, g)
                 conv(l, g)
+                start_halo(after(l), g)
                 push_sums(after(l), g)
 
                 @pl.when(g > 0)
                 def _():
                     relay_sums(after(l), g - 1)
 
-                start_halo(after(l), g)
                 return 0
 
             lax.fori_loop(0, NG, phase, 0)

time: 202 us -> 205 us (1.015)
  Pallas kernels: 199 us -> 203 us
    pallas_call x1, Pallas kernels: 196 us -> 199 us  [local_decode(): pl.pallas_call(kernel, out_shape=jax.ShapeDtypeStruct((NG, rr // RB, SUB,...]
where the time goes in v5:
time: 205 us
  Pallas kernels  203 us (99%)
    pallas_call x1, Pallas kernels, local_decode(): pl.pallas_call(kernel, out_shape=jax.ShapeDtypeStruct((NG, rr // RB, SUB,...  199 us

profile of v5, /device:TPU:0, one launch (start us, length us, event | category | flops | bytes accessed | tf_op | source)
XLA Modules:
  0.0 205.0 jit_solution(4623377919528787243)
XLA Ops:
  0.0 0.1 iota_subtract_fusion
  0.1 1.6 convolution_bitcast_fusion.wo_ref
  1.7 199.4 %decode.1.x_ref = f32[4,16,16,128]{3,2,1,0:T(8,128)} custom-call(bf16[16,4,64,8,256]{4,3,2,1,0:T(8,128)(2,1)} %bitcast.10, bf16[3,3,256,128]{3,2,1,0:T(8,128)(2,1)} %w1_ref.1, bf16[5,3,3,128,128]{4,3,2,1,0:T(8,128)(2,1)} %wr_ref.1, bf16[256,128]{1,0:T(8,128)(2,1)} %ws_ref.1, f32[3,128,128]{2,1,0:T(8,128)} %convolution_bitcast_fusion.wo_ref, ...), custom_call_target="tpu_custom_call" | custom-call | tf_op jit(solution)/shard_map/decode/pallas_call | solution.py:534
  201.1 3.9 %to_planes.1 = f32[16,3,8,256]{3,2,1,0:T(8,128)} custom-call(f32[4,16,16,128]{3,2,1,0:T(8,128)} %decode.1.x_ref, bf16[1,3]{1,0:T(2,128)(2,1)} %bitcast.11), custom_call_target="tpu_custom_call" | custom-call | tf_op jit(solution)/shard_map/to_planes/pallas_call | solution.py:574
  (1 shorter events, 0.0 us)
